TPU v7x, 256 devices: a whole 4x4x8 slice. The times are simulated.
256 devices in a mesh: gx: 4 (over z_lo), gy: 8 (over y, z_hi), gz: 8 (over x, core).
Axes of the slice: x: 4, y: 4, z: 8 (z_hi: 2, z_lo: 4; z = z_hi * 4 + z_lo), core: 2. Of those that a mesh axis runs over, the one named last changes fastest.
Arguments:
- displ: float32 [3, 4, 8, 8, 9945], P(None, 'gx', 'gy', 'gz'), may hold values from -6 to 6
- veloc: float32 [3, 4, 8, 8, 9945], P(None, 'gx', 'gy', 'gz'), may hold values from -6 to 6
- accel: float32 [3, 4, 8, 8, 9945], P(None, 'gx', 'gy', 'gz'), may hold values from -12 to 12
- node_index: int32 [4, 8, 8, 125, 128], P('gx', 'gy', 'gz'), may hold values from 0 to 9944, as said below
- inv_map: float32 [4, 8, 8, 9, 125, 128], P('gx', 'gy', 'gz'), may hold values from -1 to 2, as said below
- jac_weight: float32 [4, 8, 8, 125, 128], P('gx', 'gy', 'gz'), may hold values from 0.05 to 0.5
- lame_first: float32 [4, 8, 8, 125, 128], P('gx', 'gy', 'gz'), may hold values from 0.02 to 0.1
- shear_mod: float32 [4, 8, 8, 125, 128], P('gx', 'gy', 'gz'), may hold values from 0.02 to 0.1
- density: float32 [4, 8, 8, 125, 128], P('gx', 'gy', 'gz'), may hold values from 1 to 3
Outputs:
- displ_out: float32 [3, 4, 8, 8, 9945], P(None, 'gx', 'gy', 'gz')
- veloc_out: float32 [3, 4, 8, 8, 9945], P(None, 'gx', 'gy', 'gz')
- accel_out: float32 [3, 4, 8, 8, 9945], P(None, 'gx', 'gy', 'gz')
Inputs may be any that keep to these rules, and one draw needn't show every extreme that they name: `node_index`: on each device the element slots hold the elements of a brick of 4 x 16 x 2 elements in a drawn order, each once; element (ex, ey, ez) has its point (a, b, c) at node ((4 ex + a) * 65 + 4 ey + b) * 9 + 4 ez + c. `inv_map`: the entries with l equal to j are positive.
All inputs are finite; a program needn't handle non-finite values.
Results may differ from a plain program's by a relative error of at most 0.00024.
Values sent between devices are 32-bit elements; how exact they have to be, the bound alone decides.
No kernel may reach another device: no remote copies, remote signals or barrier semaphores. Data moves between devices by JAX's collectives and lax.ppermute only.
A program may use at most 64 MiB of HBM per device.

v0:
```python
import jax
import jax.numpy as jnp
import numpy as np
from jax import lax
from jax.sharding import PartitionSpec as P

EX = 4
EY = 16
EZ = 2


time_step = 0.1


def with_halo(block, sides, width):
    for axis, dim in sides:
        count = lax.axis_size(axis)
        forward = [(i, i + 1) for i in range(count - 1)]
        backward = [(target, source) for source, target in forward]
        low = lax.ppermute(
            lax.slice_in_dim(block, block.shape[dim] - width, None, axis=dim), axis, forward
        )
        high = lax.ppermute(lax.slice_in_dim(block, 0, width, axis=dim), axis, backward)
        block = jnp.concatenate([low, block, high], axis=dim)
    return block


def derivative_table():
    points = np.array([-1.0, -np.sqrt(3.0 / 7.0), 0.0, np.sqrt(3.0 / 7.0), 1.0])
    points_count = points.shape[0]
    weights = np.array(
        [
            1.0
            / np.prod(
                [points[source] - points[other] for other in range(points_count) if other != source]
            )
            for source in range(points_count)
        ]
    )
    deriv_table = np.zeros((points_count, points_count))
    for target in range(points_count):
        for source in range(points_count):
            if target != source:
                deriv_table[target, source] = (
                    weights[source] / weights[target] / (points[target] - points[source])
                )
        deriv_table[target, target] = -np.sum(deriv_table[target])
    return deriv_table


def split_points(grid, dim, count):
    pieces = [
        lax.slice_in_dim(grid, offset, offset + 4 * (count - 1) + 1, stride=4, axis=dim)
        for offset in range(5)
    ]
    return jnp.stack(pieces, axis=dim)


def element_view(grid):
    viewed = split_points(grid, 1, EX)
    viewed = split_points(viewed, 3, EY)
    viewed = split_points(viewed, 5, EZ)
    viewed = jnp.transpose(viewed, (0, 1, 3, 5, 2, 4, 6))
    return viewed.reshape(grid.shape[0], 125, EX * EY * EZ)


def fold_points(terms, axis):
    count = terms.shape[axis + 1]
    lead = lax.slice_in_dim(terms, 0, 4, axis=axis)
    lead = jnp.moveaxis(lead, axis, axis + 1)
    shape = lead.shape[:axis] + (4 * count,) + lead.shape[axis + 2 :]
    lead = lead.reshape(shape)
    widths = [(0, 0)] * len(shape)
    widths[axis] = (0, 1)
    lead = jnp.pad(lead, widths)
    tail = lax.slice_in_dim(terms, 4, 5, axis=axis)
    blank_shape = list(tail.shape)
    blank_shape[axis] = 3
    tail = jnp.concatenate([tail, jnp.zeros(tuple(blank_shape), terms.dtype)], axis=axis)
    tail = jnp.moveaxis(tail, axis, axis + 1).reshape(shape)
    widths[axis] = (4, 0)
    tail = lax.slice_in_dim(jnp.pad(tail, widths), 0, 4 * count + 1, axis=axis)
    return lead + tail


def fold_elements(terms):
    components = terms.shape[0]
    grid = terms.reshape(components, 5, 5, 5, EX, EY, EZ)
    grid = jnp.transpose(grid, (0, 1, 4, 2, 5, 3, 6))
    grid = fold_points(grid, 1)
    grid = fold_points(grid, 2)
    grid = fold_points(grid, 3)
    return grid.reshape(components, (4 * EX + 1) * (4 * EY + 1) * (4 * EZ + 1))


def element_terms(local, mapping, jac_weight, lame_first, shear_mod, deriv):
    highest = lax.Precision.HIGHEST
    elements = local.shape[2]
    local = local.reshape(3, 5, 5, 5, elements)
    grad_a = jnp.einsum("ap,cpbke->cabke", deriv, local, precision=highest).reshape(
        3, 125, elements
    )
    grad_b = jnp.einsum("bp,capke->cabke", deriv, local, precision=highest).reshape(
        3, 125, elements
    )
    grad_c = jnp.einsum("kp,cabpe->cabke", deriv, local, precision=highest).reshape(
        3, 125, elements
    )
    mapping = mapping.reshape(3, 3, 125, elements)
    strain_grad = (
        grad_a[:, None] * mapping[0][None]
        + grad_b[:, None] * mapping[1][None]
        + grad_c[:, None] * mapping[2][None]
    )
    divergence = strain_grad[0, 0] + strain_grad[1, 1] + strain_grad[2, 2]
    identity = jnp.eye(3, dtype=jnp.float32)[:, :, None, None]
    stress = (
        shear_mod * (strain_grad + jnp.swapaxes(strain_grad, 0, 1))
        + lame_first * divergence * identity
    )
    flux = (
        stress[:, 0][:, None] * mapping[:, 0][None]
        + stress[:, 1][:, None] * mapping[:, 1][None]
        + stress[:, 2][:, None] * mapping[:, 2][None]
    )
    flux = (jac_weight * flux).reshape(3, 3, 5, 5, 5, elements)
    terms = jnp.einsum("pa,cpbke->cabke", deriv, flux[:, 0], precision=highest)
    terms = terms + jnp.einsum("pb,capke->cabke", deriv, flux[:, 1], precision=highest)
    terms = terms + jnp.einsum("pk,cabpe->cabke", deriv, flux[:, 2], precision=highest)
    return -terms.reshape(3, 125, elements)


def fold_rim(padded, dim):
    length = padded.shape[dim] - 2
    lower = lax.slice_in_dim(padded, 0, 1, axis=dim)
    upper = lax.slice_in_dim(padded, length + 1, length + 2, axis=dim)
    inner = lax.slice_in_dim(padded, 1, length + 1, axis=dim)
    first = lax.slice_in_dim(inner, 0, 1, axis=dim) + lower
    last = lax.slice_in_dim(inner, length - 1, length, axis=dim) + upper
    middle = lax.slice_in_dim(inner, 1, length - 1, axis=dim)
    return jnp.concatenate([first, middle, last], axis=dim)


def assemble(field):
    node_x = 4 * EX + 1
    node_y = 4 * EY + 1
    node_z = 4 * EZ + 1
    components = field.shape[0]
    node_grid = field.reshape(components, node_x, node_y, node_z)
    padded = with_halo(node_grid, (("gx", 1), ("gy", 2), ("gz", 3)), 1)
    node_grid = fold_rim(fold_rim(fold_rim(padded, 1), 2), 3)
    return node_grid.reshape(components, node_x * node_y * node_z)


def body(displ, veloc, accel, node_index, inv_map, jac_weight, lame_first, shear_mod, density):
    nodes = displ.shape[4]
    elements = node_index.shape[4]
    node_x = 4 * EX + 1
    node_y = 4 * EY + 1
    node_z = 4 * EZ + 1
    deriv = jnp.asarray(derivative_table(), jnp.float32)
    position = displ.reshape(3, nodes)
    speed = veloc.reshape(3, nodes)
    acceleration = accel.reshape(3, nodes)
    corner = node_index.reshape(125, elements)[0]
    elem_x = corner // (node_y * node_z) // 4
    elem_y = corner // node_z % node_y // 4
    elem_z = corner % node_z // 4
    brick_slot = (elem_x * EY + elem_y) * EZ + elem_z
    slot_of_brick = (
        jnp.zeros((elements,), jnp.int32).at[brick_slot].set(jnp.arange(elements, dtype=jnp.int32))
    )
    mapping = inv_map.reshape(9, 125, elements)[:, :, slot_of_brick]
    weight = jac_weight.reshape(125, elements)[:, slot_of_brick]
    lame = lame_first.reshape(125, elements)[:, slot_of_brick]
    shear = shear_mod.reshape(125, elements)[:, slot_of_brick]
    dens = density.reshape(125, elements)[:, slot_of_brick]
    mass_local = fold_elements((dens * weight)[None])
    half_step = 0.5 * time_step
    half_square = 0.5 * time_step * time_step
    position = position + time_step * speed + half_square * acceleration
    speed = speed + half_step * acceleration
    local = element_view(position.reshape(3, node_x, node_y, node_z))
    force = fold_elements(element_terms(local, mapping, weight, lame, shear, deriv))
    summed = assemble(jnp.concatenate([force, mass_local], axis=0))
    force = summed[:3]
    mass = summed[3]
    acceleration = force / mass[None]
    speed = speed + half_step * acceleration
    shape = (3, 1, 1, 1, nodes)
    return (position.reshape(shape), speed.reshape(shape), acceleration.reshape(shape))


def solution(mesh):
    placed = (
        P(None, "gx", "gy", "gz", None),
        P(None, "gx", "gy", "gz", None),
        P(None, "gx", "gy", "gz", None),
        P("gx", "gy", "gz", None, None),
        P("gx", "gy", "gz", None, None, None),
        P("gx", "gy", "gz", None, None),
        P("gx", "gy", "gz", None, None),
        P("gx", "gy", "gz", None, None),
        P("gx", "gy", "gz", None, None),
    )
    return jax.shard_map(
        body,
        mesh=mesh,
        in_specs=placed,
        out_specs=(
            P(None, "gx", "gy", "gz", None),
            P(None, "gx", "gy", "gz", None),
            P(None, "gx", "gy", "gz", None),
        ),
        check_vma=False,
    )
```

profile of v0, /device:TPU:1, one launch (start us, length us, event | category | flops | bytes accessed | tf_op | source)
XLA Modules:
  0.0 168.2 jit_solution(9338076756384713582)
XLA Ops:
  14.1 2.8 %slice.246 = f32[3,5,4,16,9]{3,2,4,1,0:T(4,128)S(1)} slice(f32[3,5,4,65,9]{3,2,4,1,0:T(4,128)S(1)} %constant_dynamic-update-slice_fusion), slice={[0:3:1], [0:5:1], [0:4:1], [4:65:4], [0:9:1]} | slice | bytes 69120 | tf_op jit(solution)/shard_map/slice | solution.py:53
  16.9 6.2 %slice.245 = f32[3,5,4,16,9]{3,2,4,1,0:T(4,128)} slice(f32[3,5,4,65,9]{3,2,4,1,0:T(4,128)S(1)} %constant_dynamic-update-slice_fusion), slice={[0:3:1], [0:5:1], [0:4:1], [3:64:4], [0:9:1]} | slice | bytes 69120 | tf_op jit(solution)/shard_map/slice | solution.py:53
  23.1 6.1 %slice.244 = f32[3,5,4,16,9]{3,2,4,1,0:T(4,128)} slice(f32[3,5,4,65,9]{3,2,4,1,0:T(4,128)S(1)} %constant_dynamic-update-slice_fusion), slice={[0:3:1], [0:5:1], [0:4:1], [2:63:4], [0:9:1]} | slice | bytes 69120 | tf_op jit(solution)/shard_map/slice | solution.py:53
  29.2 6.1 %slice.243 = f32[3,5,4,16,9]{3,2,4,1,0:T(4,128)} slice(f32[3,5,4,65,9]{3,2,4,1,0:T(4,128)S(1)} %constant_dynamic-update-slice_fusion), slice={[0:3:1], [0:5:1], [0:4:1], [1:62:4], [0:9:1]} | slice | bytes 69120 | tf_op jit(solution)/shard_map/slice | solution.py:53
  35.4 6.1 %slice.242 = f32[3,5,4,16,9]{3,2,4,1,0:T(4,128)} slice(f32[3,5,4,65,9]{3,2,4,1,0:T(4,128)S(1)} %constant_dynamic-update-slice_fusion), slice={[0:3:1], [0:5:1], [0:4:1], [0:61:4], [0:9:1]} | slice | bytes 69120 | tf_op jit(solution)/shard_map/slice | solution.py:53
  45.9 1.6 slice_bitcast_fusion.1
  47.5 3.6 %copy.227 = f32[1,4,4,5,16,5,2]{4,2,1,6,5,3,0:T(4,128)} copy(f32[1,4,4,5,16,5,2]{5,3,2,6,4,1,0:T(8,128)} %slice_bitcast_fusion.1) | data formatting | bytes 102400 | tf_op jit(solution)/shard_map/transpose | solution.py:70
  51.4 2.1 %copy.228 = f32[1,4,4,5,16,5,2]{4,2,1,6,5,3,0:T(4,128)} copy(f32[1,4,4,5,16,5,2]{5,3,2,6,4,1,0:T(8,128)S(1)} %pad_bitcast_fusion.1) | data formatting | bytes 102400 | tf_op jit(solution)/shard_map/transpose | solution.py:80
  57.4 6.9 %copy.182 = f32[3,5,5,5,4,16,2]{3,6,5,4,2,1,0:T(2,128)} copy(f32[3,5,5,5,4,16,2]{5,4,6,1,0,2,3:T(4,128)S(1)} %bitcast.191) | data formatting | bytes 384000 | tf_op jit(solution)/shard_map/transpose | solution.py:63
  64.4 4.7 %copy.188 = f32[3,5,5,5,128]{4,2,3,1,0:T(8,128)S(1)} copy(f32[3,5,5,5,128]{3,4,2,1,0:T(8,128)} %bitcast.172) | data formatting | bytes 384000 | tf_op jit(solution)/shard_map/reshape;reshape | solution.py:99
  69.1 4.9 %copy.183 = f32[3,5,5,5,128]{4,1,3,2,0:T(8,128)S(1)} copy(f32[3,5,5,5,128]{3,4,2,1,0:T(8,128)} %bitcast.173) | data formatting | bytes 384000 | tf_op jit(solution)/shard_map/reshape;reshape | solution.py:99
  78.4 6.8 %convolution_bitcast_fusion = f32[3,5,5,5,128]{4,3,2,1,0:T(8,128)S(1)} fusion(f32[3,5,5,5,128]{3,4,2,1,0:T(8,128)} %bitcast.174, f32[5,5,1,1,1]{1,0,4,3,2:T(8,128)S(1)} %copy-done.18), kind=kOutput, calls=%fused_computation.13 | convolution fusion | flops 2880000 | bytes 384100 | tf_op jit(solution)/shard_map/kp,cabpe->cabke/dot_general | solution.py:106
  90.0 3.2 %copy.219 = f32[3,5,5,5,128]{3,4,2,1,0:T(8,128)} copy(f32[3,5,5,5,128]{4,1,3,2,0:T(8,128)S(1)} %fusion.2) | data formatting | bytes 384000 | tf_op jit(solution)/shard_map/neg | solution.py:130
  94.6 7.2 %slice_bitcast_fusion = f32[3,4,4,5,16,5,2]{5,6,4,1,3,2,0:T(2,128)} fusion(f32[3,5,4,5,16,5,2]{5,6,4,2,3,1,0:T(2,128)} %bitcast.176), kind=kLoop, calls=%fused_computation.6 | loop fusion | bytes 307200 | tf_op jit(solution)/shard_map/transpose | solution.py:70
  101.7 5.8 %copy.220 = f32[3,4,4,5,16,5,2]{4,2,1,6,5,3,0:T(4,128)S(1)} copy(f32[3,4,4,5,16,5,2]{5,6,4,1,3,2,0:T(2,128)} %slice_bitcast_fusion) | data formatting | bytes 307200 | tf_op jit(solution)/shard_map/transpose | solution.py:70
  107.6 3.9 %pad_bitcast_fusion = f32[3,4,4,5,16,5,2]{5,6,4,1,3,2,0:T(2,128)} fusion(f32[3,1,4,5,16,5,2]{5,6,4,2,3,1,0:T(2,128)S(1)} %slice.335), kind=kLoop, calls=%fused_computation.7 | loop fusion | bytes 192000 | tf_op jit(solution)/shard_map/transpose | solution.py:80
  111.5 5.8 %copy.221 = f32[3,4,4,5,16,5,2]{4,2,1,6,5,3,0:T(4,128)S(1)} copy(f32[3,4,4,5,16,5,2]{5,6,4,1,3,2,0:T(2,128)} %pad_bitcast_fusion) | data formatting | bytes 307200 | tf_op jit(solution)/shard_map/transpose | solution.py:80
  122.5 4.4 %collective-permute-start = (f32[4,1,65,9]{2,3,1,0:T(8,128)S(1)}, f32[4,1,65,9]{2,3,1,0:T(8,128)S(1)}, u32[]{:S(2)}, u32[]{:S(2)}) collective-permute-start(f32[4,1,65,9]{2,3,1,0:T(8,128)S(1)} %get-tuple-element.42), channel_id=1, source_target_pairs={{0,64},{64,128},{128,192},{1,65},{65,129},{129,193},{2,66},{66,130... | collective-permute-start | bytes 28088 | tf_op jit(solution)/shard_map/ppermute | solution.py:20
  128.1 3.5 %collective-permute-done.1 = f32[4,1,65,9]{2,3,1,0:T(8,128)S(1)} collective-permute-done((f32[4,1,65,9]{2,3,1,0:T(8,128)S(1)}, f32[4,1,65,9]{2,3,1,0:T(8,128)S(1)}, u32[]{:S(2)}, u32[]{:S(2)}) %collective-permute-start.1) | collective-permute-done | bytes 9392 | tf_op jit(solution)/shard_map/ppermute | solution.py:23
  132.3 7.7 %collective-permute-start.2 = (f32[4,19,1,9]{1,0,3,2:T(4,128)S(1)}, f32[4,19,1,9]{1,0,3,2:T(4,128)S(1)}, u32[]{:S(2)}, u32[]{:S(2)}) collective-permute-start(f32[4,19,1,9]{1,0,3,2:T(4,128)S(1)} %copy.233), channel_id=1, source_target_pairs={{0,8},{8,16},{16,24},{24,32},{32,40},{40,48},{48,56},{1,9},{9,17},... | collective-permute-start | bytes 8216 | tf_op jit(solution)/shard_map/ppermute | solution.py:20
  142.2 6.6 %collective-permute-done.3 = f32[4,19,1,9]{1,0,3,2:T(4,128)S(1)} collective-permute-done((f32[4,19,1,9]{1,0,3,2:T(4,128)S(1)}, f32[4,19,1,9]{1,0,3,2:T(4,128)S(1)}, u32[]{:S(2)}, u32[]{:S(2)}) %collective-permute-start.3) | collective-permute-done | bytes 2768 | tf_op jit(solution)/shard_map/ppermute | solution.py:23
  149.7 6.5 %collective-permute-start.4 = (f32[4,19,67,1]{2,3,1,0:T(1,128)S(1)}, f32[4,19,67,1]{2,3,1,0:T(1,128)S(1)}, u32[]{:S(2)}, u32[]{:S(2)}) collective-permute-start(f32[4,19,67,1]{2,3,1,0:T(1,128)S(1)} %get-tuple-element.21), channel_id=1, source_target_pairs={{0,1},{1,2},{2,3},{3,4},{4,5},{5,6},{6,7},{8,9},{9,10},{10,11},{11... | collective-permute-start | bytes 61112 | tf_op jit(solution)/shard_map/ppermute | solution.py:20
  156.3 1.9 %collective-permute-start.5 = (f32[4,19,67,1]{2,3,1,0:T(1,128)S(1)}, f32[4,19,67,1]{2,3,1,0:T(1,128)S(1)}, u32[]{:S(2)}, u32[]{:S(2)}) collective-permute-start(f32[4,19,67,1]{2,3,1,0:T(1,128)S(1)} %get-tuple-element.22), channel_id=1, source_target_pairs={{1,0},{2,1},{3,2},{4,3},{5,4},{6,5},{7,6},{9,8},{10,9},{11,10},{12... | collective-permute-start | bytes 61112 | tf_op jit(solution)/shard_map/ppermute | solution.py:23
  158.2 3.4 %collective-permute-done.5 = f32[4,19,67,1]{2,3,1,0:T(1,128)S(1)} collective-permute-done((f32[4,19,67,1]{2,3,1,0:T(1,128)S(1)}, f32[4,19,67,1]{2,3,1,0:T(1,128)S(1)}, u32[]{:S(2)}, u32[]{:S(2)}) %collective-permute-start.5) | collective-permute-done | bytes 20400 | tf_op jit(solution)/shard_map/ppermute | solution.py:23
  (197 shorter events, 48.5 us)
Async XLA Ops:
  2.9 39.4 %copy-start.24 = (s32[1024]{0:T(1024)}, s32[1024]{0:T(1024)S(1)}, u32[]{:S(2)}) copy-start(s32[1024]{0:T(1024)S(1)} %pad_clamp_fusion) | copy-start | bytes 12292
  5.3 1.3 copy-start.11
  5.3 1.3 copy-start.13
  5.3 1.3 copy-start.19
  9.9 3.7 %copy-start.1 = (f32[3,1,4,65,9]{4,3,2,0,1:T(8,128)S(1)}, f32[3,1,4,65,9]{4,3,2,0,1:T(8,128)}, u32[]{:S(2)}) copy-start(f32[3,1,4,65,9]{4,3,2,0,1:T(8,128)} %get-tuple-element.19) | copy-start | bytes 84244
  14.0 27.4 %copy-start.20 = (f32[1,1,1,125,128]{4,2,3,1,0:T(1,128)S(1)}, f32[1,1,1,125,128]{4,2,3,1,0:T(1,128)}, u32[]{:S(2)}) copy-start(f32[1,1,1,125,128]{4,2,3,1,0:T(1,128)} %param.15) | copy-start | bytes 192004
  16.9 25.3 %copy-start.21 = (f32[1,1,1,125,128]{4,2,3,1,0:T(1,128)S(1)}, f32[1,1,1,125,128]{4,2,3,1,0:T(1,128)}, u32[]{:S(2)}) copy-start(f32[1,1,1,125,128]{4,2,3,1,0:T(1,128)} %param.18) | copy-start | bytes 192004
  47.5 3.6 %copy-start = (f32[1,1,4,5,16,5,2]{5,3,1,6,4,2,0:T(8,128)S(1)}, f32[1,1,4,5,16,5,2]{5,3,1,6,4,2,0:T(8,128)}, u32[]{:S(2)}) copy-start(f32[1,1,4,5,16,5,2]{5,3,1,6,4,2,0:T(8,128)} %slice.341) | copy-start | bytes 38404
  51.4 2.1 %copy-start.2 = (f32[1,4,4,5,16,5,2]{4,2,1,6,5,3,0:T(4,128)S(1)}, f32[1,4,4,5,16,5,2]{4,2,1,6,5,3,0:T(4,128)}, u32[]{:S(2)}) copy-start(f32[1,4,4,5,16,5,2]{4,2,1,6,5,3,0:T(4,128)} %copy.227) | copy-start | bytes 153604
  55.0 1.8 %copy-start.7 = (f32[3,5,4,16,9]{3,2,4,1,0:T(4,128)S(1)}, f32[3,5,4,16,9]{3,2,4,1,0:T(4,128)}, u32[]{:S(2)}) copy-start(f32[3,5,4,16,9]{3,2,4,1,0:T(4,128)} %slice.242) | copy-start | bytes 103684
  55.0 1.8 %copy-start.6 = (f32[3,5,4,16,9]{3,2,4,1,0:T(4,128)S(1)}, f32[3,5,4,16,9]{3,2,4,1,0:T(4,128)}, u32[]{:S(2)}) copy-start(f32[3,5,4,16,9]{3,2,4,1,0:T(4,128)} %slice.243) | copy-start | bytes 103684
  55.4 1.5 copy-start.5
  55.4 1.6 copy-start.4
  69.0 5.1 %copy-start.22 = (f32[1,1,1,125,128]{4,2,3,1,0:T(1,128)S(1)}, f32[1,1,1,125,128]{4,2,3,1,0:T(1,128)}, u32[]{:S(2)}) copy-start(f32[1,1,1,125,128]{4,2,3,1,0:T(1,128)} %param.16) | copy-start | bytes 192004
  69.1 6.5 %copy-start.23 = (f32[1,1,1,125,128]{4,2,3,1,0:T(1,128)S(1)}, f32[1,1,1,125,128]{4,2,3,1,0:T(1,128)}, u32[]{:S(2)}) copy-start(f32[1,1,1,125,128]{4,2,3,1,0:T(1,128)} %param.17) | copy-start | bytes 192004
  74.0 3.3 %copy-start.10 = (f32[3,125,128]{1,0,2:T(4,128)S(1)}, f32[3,125,128]{1,0,2:T(4,128)}, u32[]{:S(2)}) copy-start(f32[3,125,128]{1,0,2:T(4,128)} %get-tuple-element.25) | copy-start | bytes 576004
  75.7 1.7 %copy-start.9 = (f32[3,125,128]{1,0,2:T(4,128)S(1)}, f32[3,125,128]{1,0,2:T(4,128)}, u32[]{:S(2)}) copy-start(f32[3,125,128]{1,0,2:T(4,128)} %get-tuple-element.26) | copy-start | bytes 576004
  120.2 1.1 copy-start.15
  122.5 5.7 %collective-permute-start = (f32[4,1,65,9]{2,3,1,0:T(8,128)S(1)}, f32[4,1,65,9]{2,3,1,0:T(8,128)S(1)}, u32[]{:S(2)}, u32[]{:S(2)}) collective-permute-start(f32[4,1,65,9]{2,3,1,0:T(8,128)S(1)} %get-tuple-element.42), channel_id=1, source_target_pairs={{0,64},{64,128},{128,192},{1,65},{65,129},{129,193},{2,66},{66,130... | collective-permute-start | bytes 28088 | tf_op jit(solution)/shard_map/ppermute | solution.py:20
  126.8 4.9 %collective-permute-start.1 = (f32[4,1,65,9]{2,3,1,0:T(8,128)S(1)}, f32[4,1,65,9]{2,3,1,0:T(8,128)S(1)}, u32[]{:S(2)}, u32[]{:S(2)}) collective-permute-start(f32[4,1,65,9]{2,3,1,0:T(8,128)S(1)} %get-tuple-element.43), channel_id=1, source_target_pairs={{64,0},{128,64},{192,128},{65,1},{129,65},{193,129},{66,2},{130,66... | collective-permute-start | bytes 28088 | tf_op jit(solution)/shard_map/ppermute | solution.py:23
  132.3 9.4 %collective-permute-start.2 = (f32[4,19,1,9]{1,0,3,2:T(4,128)S(1)}, f32[4,19,1,9]{1,0,3,2:T(4,128)S(1)}, u32[]{:S(2)}, u32[]{:S(2)}) collective-permute-start(f32[4,19,1,9]{1,0,3,2:T(4,128)S(1)} %copy.233), channel_id=1, source_target_pairs={{0,8},{8,16},{16,24},{24,32},{32,40},{40,48},{48,56},{1,9},{9,17},... | collective-permute-start | bytes 8216 | tf_op jit(solution)/shard_map/ppermute | solution.py:20
  140.4 8.4 %collective-permute-start.3 = (f32[4,19,1,9]{1,0,3,2:T(4,128)S(1)}, f32[4,19,1,9]{1,0,3,2:T(4,128)S(1)}, u32[]{:S(2)}, u32[]{:S(2)}) collective-permute-start(f32[4,19,1,9]{1,0,3,2:T(4,128)S(1)} %copy.234), channel_id=1, source_target_pairs={{8,0},{16,8},{24,16},{32,24},{40,32},{48,40},{56,48},{9,1},{17,9},... | collective-permute-start | bytes 8216 | tf_op jit(solution)/shard_map/ppermute | solution.py:23
  149.7 8.5 %collective-permute-start.4 = (f32[4,19,67,1]{2,3,1,0:T(1,128)S(1)}, f32[4,19,67,1]{2,3,1,0:T(1,128)S(1)}, u32[]{:S(2)}, u32[]{:S(2)}) collective-permute-start(f32[4,19,67,1]{2,3,1,0:T(1,128)S(1)} %get-tuple-element.21), channel_id=1, source_target_pairs={{0,1},{1,2},{2,3},{3,4},{4,5},{5,6},{6,7},{8,9},{9,10},{10,11},{11... | collective-permute-start | bytes 61112 | tf_op jit(solution)/shard_map/ppermute | solution.py:20
  156.3 5.3 %collective-permute-start.5 = (f32[4,19,67,1]{2,3,1,0:T(1,128)S(1)}, f32[4,19,67,1]{2,3,1,0:T(1,128)S(1)}, u32[]{:S(2)}, u32[]{:S(2)}) collective-permute-start(f32[4,19,67,1]{2,3,1,0:T(1,128)S(1)} %get-tuple-element.22), channel_id=1, source_target_pairs={{1,0},{2,1},{3,2},{4,3},{5,4},{6,5},{7,6},{9,8},{10,9},{11,10},{12... | collective-permute-start | bytes 61112 | tf_op jit(solution)/shard_map/ppermute | solution.py:23
  (8 other events, 7.3 us)
where the time goes:
time: 169 us; the launch traced here: 168 us
  local copies, waits for them, and re-layouts  113 us (67%)
  starting transfers between devices  23.1 us (14%)
  waiting for transfers between devices  13.5 us (8%)
  matrix products  8.97 us (5%)
  other arithmetic  8.09 us (5%)
  between operations  1.72 us (1%)
    slice x5, local copies, waits for them, and re-layouts, split_points(): lax.slice_in_dim(grid, offset, offset + 4 * (count - 1) + 1, stride=4, ax...  27.4 us
    transpose x12, local copies, waits for them, and re-layouts, fold_points(): lead = jnp.moveaxis(lead, axis, axis + 1)  21 us
    ppermute x3, starting transfers between devices, with_halo(): lax.ppermute(lax.slice_in_dim(block, block.shape[dim] - width, None, axis...  18.6 us
    transpose x12, local copies, waits for them, and re-layouts, fold_points(): tail = jnp.moveaxis(tail, axis, axis + 1).reshape(shape)  14.2 us
    ppermute x3, waiting for transfers between devices, with_halo(): lax.ppermute(lax.slice_in_dim(block, 0, width, axis=dim), axis, backward)  13.5 us
    another operation x2, local copies, waits for them, and re-layouts, element_terms(): local = local.reshape(3, 5, 5, 5, elements)  9.54 us
    transpose x1, local copies, waits for them, and re-layouts, element_view(): viewed = jnp.transpose(viewed, (0, 1, 3, 5, 2, 4, 6))  6.94 us
    dot_general x1, matrix products, element_terms(): jnp.einsum('kp,cabpe->cabke', deriv, local, precision=highest)  6.76 us
  transfers between devices with their start and end apart: 6, of which 3 were waited for; matrix products, arithmetic and copies ran while one was open for 1% of the time, Pallas kernels for 0%

commit v1 on v0

v1 whole, which is shorter than its diff:
```python
import functools

import jax
import jax.numpy as jnp
import numpy as np
from jax import lax
from jax.experimental import pallas as pl
from jax.experimental.pallas import tpu as pltpu
from jax.sharding import PartitionSpec as P

EX = 4
EY = 16
EZ = 2
NX = 4 * EX + 1
NY = 4 * EY + 1
NZ = 4 * EZ + 1
NODES = NX * NY * NZ
ROW = NY * NZ
XPAD = 24
FROWS = 960

time_step = 0.1
HALF = 0.5 * time_step
HALF_SQ = 0.5 * time_step * time_step
F32 = jnp.float32
BF16 = jnp.bfloat16
VMEM = pl.BlockSpec(memory_space=pltpu.VMEM)
HBM = pl.BlockSpec(memory_space=pltpu.HBM)


def derivative_table():
    points = np.array([-1.0, -np.sqrt(3.0 / 7.0), 0.0, np.sqrt(3.0 / 7.0), 1.0])
    count = points.shape[0]
    weights = np.array(
        [
            1.0 / np.prod([points[s] - points[o] for o in range(count) if o != s])
            for s in range(count)
        ]
    )
    table = np.zeros((count, count))
    for target in range(count):
        for source in range(count):
            if target != source:
                table[target, source] = (
                    weights[source] / weights[target] / (points[target] - points[source])
                )
        table[target, target] = -np.sum(table[target])
    return table


def operator_tables():
    table = derivative_table().astype(np.float32).astype(np.float64)
    eye = np.eye(5)
    full = np.zeros((3, 128, 128))
    full[0, :125, :125] = np.kron(np.kron(table, eye), eye)
    full[1, :125, :125] = np.kron(np.kron(eye, table), eye)
    full[2, :125, :125] = np.kron(np.kron(eye, eye), table)
    forward = full.reshape(384, 128)
    backward = -np.transpose(full, (2, 0, 1)).reshape(128, 384)
    out = []
    for matrix in (forward, backward):
        high = matrix.astype(np.float32).astype(jnp.bfloat16)
        low = (matrix - high.astype(np.float64)).astype(np.float32).astype(jnp.bfloat16)
        out.append(np.concatenate([high, low], axis=0))
    return out


def split(value):
    high = value.astype(BF16)
    return high, (value - high.astype(F32)).astype(BF16)


def dot(lhs, rhs):
    return lax.dot_general(lhs, rhs, (((1,), (0,)), ((), ())), preferred_element_type=F32)


def take(value, index):
    return jnp.take_along_axis(value, index, axis=1, mode="promise_in_bounds")


def lanes(shape=(8, 128)):
    return lax.broadcasted_iota(jnp.int32, shape, len(shape) - 1)


def force_kernel(
    d_hbm, v_hbm, a_hbm, n_hbm, m_hbm, j_hbm, l_hbm, s_hbm, r_hbm, fw_hbm, bw_hbm,
    t_ref, o_ref, y_ref, vh_ref, d_out,
    d_s, v_s, a_s, n_s, m_s, j_s, l_s, s_s, r_s, fw_s, bw_s,
    pos_s, grid_s, nodal_s, local_s, grad_s, fluxh_s, fluxl_s, sems,
):
    copies = []
    moves = [(d_hbm, d_s), (v_hbm, v_s), (a_hbm, a_s), (n_hbm.at[pl.ds(0, 1)], n_s), (fw_hbm, fw_s)]
    for k in range(9):
        moves.append((m_hbm.at[pl.ds(125 * k, 125), 0], m_s.at[k, pl.ds(0, 125)]))
    for src, dst in ((j_hbm, j_s), (l_hbm, l_s), (s_hbm, s_s), (r_hbm, r_s)):
        moves.append((src.at[pl.ds(0, 125), 0], dst.at[pl.ds(0, 125)]))
    moves.append((bw_hbm, bw_s))
    for at, (src, dst) in enumerate(moves):
        copy = pltpu.make_async_copy(src, dst, sems.at[at])
        copy.start()
        copies.append(copy)
    for at in range(4):
        copies[at].wait()
    accel = a_s[...]
    veloc = v_s[...]
    pos_s[...] = d_s[...] + time_step * veloc + HALF_SQ * accel
    vh_ref[...] = veloc + HALF * accel
    out_copy = pltpu.make_async_copy(pos_s, d_out, sems.at[19])
    out_copy.start()
    lane = lanes()

    corner = jnp.broadcast_to(n_s[0], (8, 128))
    elem_x = (
        (corner >= 2340).astype(jnp.int32)
        + (corner >= 4680).astype(jnp.int32)
        + (corner >= 7020).astype(jnp.int32)
    )
    rest = corner - 2340 * elem_x
    elem_y = jnp.floor((rest.astype(F32) + 0.5) * (1.0 / 36.0)).astype(jnp.int32)
    elem_z = (rest - 36 * elem_y) >> 2
    group = elem_x * 2 + elem_z
    brick = (group * 16 + elem_y).astype(F32)
    column = jnp.broadcast_to(brick[0:1], (128, 128)).T
    hit = column == lanes((128, 128)).astype(F32)
    slot_index = lax.broadcasted_iota(jnp.int32, (128, 128), 0).astype(F32)
    slot_of = jnp.sum(jnp.where(hit, slot_index, 0.0), axis=0, keepdims=True)
    slot_of = jnp.broadcast_to(slot_of, (8, 128)).astype(jnp.int32)

    for m in range(3):
        for x in range(NX):
            grid_s[m, x : x + 1, :ROW] = pos_s[m, :, pl.ds(ROW * x, ROW)]
    for m in range(3):
        for tile in range(3):
            parts = [grid_s[m, 8 * tile : 8 * tile + 8, 128 * v : 128 * v + 128] for v in range(5)]
            for z in range(NZ):
                at = 9 * lane + z
                low = at & 127
                high = at >> 7
                got = take(parts[0], low)
                for v in range(1, 5):
                    got = jnp.where(high == v, take(parts[v], low), got)
                nodal_s[m, z, 8 * tile : 8 * tile + 8, :] = got

    masks = [group == g for g in range(8)]
    indices = [4 * elem_y + b for b in range(5)]
    for m in range(3):
        local_s[m, 120:128, :] = jnp.zeros((8, 128), F32)
        for c in range(5):
            parts = [
                nodal_s[m, 4 * (g % 2) + c, 4 * (g // 2) : 4 * (g // 2) + 8, :] for g in range(8)
            ]
            for b in range(5):
                got = take(parts[0], indices[b])
                for g in range(1, 8):
                    got = jnp.where(masks[g], take(parts[g], indices[b]), got)
                local_s[m, pl.ds(5 * b + c, 5, stride=25), :] = got[:5]

    copies[4].wait()
    local = jnp.concatenate([local_s[m] for m in range(3)], axis=1)
    high, low = split(local)
    both = dot(fw_s[...], high)
    grad_s[...] = both[:384] + both[384:] + dot(fw_s[0:384, :], low)

    for at in range(5, 18):
        copies[at].wait()
    for chunk in range(8):
        at = 16 * chunk
        rows = slice(at, at + 16)
        g = [
            [grad_s[128 * l + at : 128 * l + at + 16, 128 * c : 128 * c + 128] for c in range(3)]
            for l in range(3)
        ]
        mp = [[m_s[3 * l + j, rows, :] for j in range(3)] for l in range(3)]
        gr = [
            [g[0][c] * mp[0][j] + g[1][c] * mp[1][j] + g[2][c] * mp[2][j] for j in range(3)]
            for c in range(3)
        ]
        mu = s_s[rows, :]
        trace = l_s[rows, :] * (gr[0][0] + gr[1][1] + gr[2][2])
        weight = j_s[rows, :]
        stress = [[None] * 3 for _ in range(3)]
        for c in range(3):
            for j in range(c, 3):
                value = mu * (gr[c][j] + gr[j][c])
                stress[c][j] = stress[j][c] = value + trace if c == j else value
        keep = lax.broadcasted_iota(jnp.int32, (16, 128), 0) < 125 - at
        mass = r_s[rows, :] * weight
        t_ref[3, rows, :] = jnp.where(keep, mass, 0.0) if chunk == 7 else mass
        for l in range(3):
            for c in range(3):
                flux = weight * (
                    stress[c][0] * mp[l][0] + stress[c][1] * mp[l][1] + stress[c][2] * mp[l][2]
                )
                if chunk == 7:
                    flux = jnp.where(keep, flux, 0.0)
                high, low = split(flux)
                to = slice(128 * l + at, 128 * l + at + 16)
                cols = slice(128 * c, 128 * c + 128)
                fluxh_s[to, cols] = high
                fluxl_s[to, cols] = low

    copies[18].wait()
    both = dot(bw_s[...], fluxh_s[...])
    terms = both[:128] + both[128:] + dot(bw_s[0:128, :], fluxl_s[...])
    for m in range(3):
        t_ref[m, 0:128, :] = terms[:, 128 * m : 128 * m + 128]
    for m in range(4):
        t_ref[m, 128:200, :] = jnp.zeros((72, 128), F32)
    o_ref[...] = slot_of

    edge = take(slot_of, 16 * (lane & 7) + 15 * ((lane >> 3) & 1))
    second = ((lane >> 3) & 1) == 1
    packs = []
    for q in range(3):
        pack = jnp.zeros((8, 128), F32)
        for k in range(8 * q, min(8 * q + 8, 20)):
            m, c = divmod(k, 5)
            got = jnp.where(
                second,
                take(t_ref[m, pl.ds(20 + c, 8, stride=25), :], edge),
                take(t_ref[m, pl.ds(c, 8, stride=25), :], edge),
            )
            pack = jnp.where((lane >> 4) == k - 8 * q, got, pack)
        packs.append(pack)
    even = 1 - lax.axis_index("gy") % 2
    upper = (lane >= 64).astype(jnp.int32)
    face = upper + even - 2 * upper * even
    plane = lane - 64 * upper
    comp = (
        (plane >= 9).astype(jnp.int32)
        + (plane >= 18).astype(jnp.int32)
        + (plane >= 27).astype(jnp.int32)
    )
    z = plane - 9 * comp
    row = lax.broadcasted_iota(jnp.int32, (8, 128), 0)
    zero = jnp.zeros((8, 128), F32)
    parts = []
    for x in range(4):
        total = zero
        for h in range(2):
            c = z - 4 * h
            good = (c >= 0) & (c <= 4) & (plane < 36)
            k = 5 * comp + c
            at = (16 * (k & 7) + 8 * face + 2 * x + h) & 127
            for q in range(3):
                total = total + jnp.where(good & ((k >> 3) == q), take(packs[q], at), zero)
        parts.append(total)
    stack_rows(parts, row, zero, y_ref, 0)
    out_copy.wait()


def stack_rows(parts, row, zero, out_ref, at):
    second = pltpu.roll(parts[1], 4, 0)
    fourth = pltpu.roll(parts[3], 4, 0)
    out_ref[at : at + 8, :] = parts[0] + jnp.where(row >= 4, second, zero)
    out_ref[at + 8 : at + 16, :] = (
        parts[2] + jnp.where(row < 4, second, zero) + jnp.where(row >= 4, fourth, zero)
    )
    out_ref[at + 16 : at + 24, :] = jnp.where(row < 4, fourth, zero)


def field_kernel(t_ref, o_ref, f_ref):
    slot_of = o_ref[...]
    lane = lanes()
    gathers = []
    for g in range(8):
        base = 16 * g + (lane >> 2)
        gathers.append(
            (take(slot_of, jnp.minimum(base, 127)), take(slot_of, jnp.clip(base - 1, 0, 127)))
        )
    quarter = lane & 3
    inside = lane < 64
    firsts = [(quarter == b) & inside for b in range(4)]
    lasts = (quarter == 0) & (lane >= 4) & (lane < 68)
    row = lax.broadcasted_iota(jnp.int32, (8, 128), 0)
    zero = jnp.zeros((8, 128), F32)
    for m in range(4):
        planes = {}
        for c in range(5):
            parts = [t_ref[m, pl.ds(5 * b + c, 8, stride=25), :] for b in range(5)]
            for g in range(8):
                at, before = gathers[g]
                got = jnp.where(firsts[0], take(parts[0], at), zero)
                for b in range(1, 4):
                    got = jnp.where(firsts[b], take(parts[b], at), got)
                got = got + jnp.where(lasts, take(parts[4], before), zero)
                key = (4 * (g % 2) + c, g // 2)
                planes[key] = planes[key] + got if key in planes else got
        for z in range(NZ):
            stack_rows([planes[(z, x)] for x in range(4)], row, zero, f_ref, (m * 9 + z) * XPAD)
    f_ref[36 * XPAD : FROWS, :] = jnp.zeros((FROWS - 36 * XPAD, 128), F32)


def y_faces(ya, yb):
    at = lax.axis_index("gy")
    odd = at % 2 == 1
    outer = (at > 0) & (at < lax.axis_size("gy") - 1)
    far = jnp.where(outer, yb, 0.0)
    return jnp.where(odd, ya, far), jnp.where(odd, far, ya)


def x_kernel(ya_ref, yb_ref, f_ref, xa_ref, xb_ref):
    pad = jnp.zeros((128 - XPAD, 128), F32)
    near = jnp.concatenate([ya_ref[...], pad], axis=0).T[0:40]
    far = jnp.concatenate([yb_ref[...], pad], axis=0).T[64:104]
    lo, hi = y_faces(near, far)
    lane = lanes((40, 128))

    def face(x):
        return (
            f_ref[pl.ds(x, 40, stride=XPAD), :]
            + jnp.where(lane == 0, pltpu.roll(lo, (128 - x) % 128, 1) if x else lo, 0.0)
            + jnp.where(lane == 64, pltpu.roll(hi, 64 - x, 1), 0.0)
        )

    first = face(0)
    last = face(16)
    odd = lax.axis_index("gx") % 2 == 1
    xa_ref[...] = jnp.where(odd, first, last)
    xb_ref[...] = jnp.where(odd, last, first)


def y_kernel(ya_ref, yb_ref, f_in, f_ref):
    lane = lanes()
    for tile in range(3):
        rows = slice(8 * tile, 8 * tile + 8)
        lo, hi = y_faces(ya_ref[rows, :], pltpu.roll(yb_ref[rows, :], 64, 1))
        for plane in range(36):
            to = slice(plane * XPAD + 8 * tile, plane * XPAD + 8 * tile + 8)
            low = pltpu.roll(lo, 128 - plane, 1) if plane else lo
            f_ref[to, :] = (
                f_in[to, :]
                + jnp.where(lane == 0, low, 0.0)
                + jnp.where(lane == 64, pltpu.roll(hi, (64 - plane) % 128, 1), 0.0)
            )


def z_kernel(xa_ref, xb_ref, f_in, f_ref, za_ref, zb_ref):
    at = lax.axis_index("gx")
    odd = at % 2 == 1
    outer = (at > 0) & (at < lax.axis_size("gx") - 1)
    near = xa_ref[0:36, :]
    far = jnp.where(outer, xb_ref[0:36, :], 0.0)
    f_ref[0 : 36 * XPAD, :] = f_in[0 : 36 * XPAD, :]
    f_ref[pl.ds(0, 36, stride=XPAD), :] = f_in[pl.ds(0, 36, stride=XPAD), :] + jnp.where(
        odd, near, far
    )
    f_ref[pl.ds(16, 36, stride=XPAD), :] = f_in[pl.ds(16, 36, stride=XPAD), :] + jnp.where(
        odd, far, near
    )
    odd = lax.axis_index("gz") % 2 == 1
    for m in range(4):
        at = m * 9 * XPAD
        first = f_ref[at : at + XPAD, :]
        last = f_ref[at + 8 * XPAD : at + 9 * XPAD, :]
        za_ref[XPAD * m : XPAD * m + XPAD, :] = jnp.where(odd, first, last)
        zb_ref[XPAD * m : XPAD * m + XPAD, :] = jnp.where(odd, last, first)


def end_kernel(za_ref, zb_ref, f_ref, vh_ref, v_out, a_out, a_s, v_s, acc_s, grid_s, sems):
    at = lax.axis_index("gz")
    odd = at % 2 == 1
    outer = (at > 0) & (at < lax.axis_size("gz") - 1)
    lane = lanes()

    def added(m, z, tile):
        value = f_ref[(m * 9 + z) * XPAD + 8 * tile : (m * 9 + z) * XPAD + 8 * tile + 8, :]
        if z in (0, 8):
            rows = slice(XPAD * m + 8 * tile, XPAD * m + 8 * tile + 8)
            near = za_ref[rows, :]
            far = jnp.where(outer, zb_ref[rows, :], 0.0)
            value = value + (jnp.where(odd, near, far) if z == 0 else jnp.where(odd, far, near))
        return value

    for z in range(NZ):
        for tile in range(3):
            mass = added(3, z, tile)
            for m in range(3):
                acc_s[m, z, 8 * tile : 8 * tile + 8, :] = added(m, z, tile) / mass
    for m in range(3):
        for tile in range(3):
            parts = [acc_s[m, z, 8 * tile : 8 * tile + 8, :] for z in range(NZ)]
            for v in range(5):
                at = lane + 128 * v
                y = jnp.floor((at.astype(F32) + 0.5) * (1.0 / 9.0)).astype(jnp.int32)
                z_of = at - 9 * y
                got = take(parts[0], y)
                for z in range(1, NZ):
                    got = jnp.where(z_of == z, take(parts[z], y), got)
                grid_s[m, 8 * tile : 8 * tile + 8, 128 * v : 128 * v + 128] = got
    for m in range(3):
        for x in range(NX):
            a_s[m, :, pl.ds(ROW * x, ROW)] = grid_s[m, x : x + 1, :ROW]
    a_copy = pltpu.make_async_copy(a_s, a_out, sems.at[0])
    a_copy.start()
    v_s[...] = vh_ref[...] + HALF * a_s[...]
    v_copy = pltpu.make_async_copy(v_s, v_out, sems.at[1])
    v_copy.start()
    a_copy.wait()
    v_copy.wait()


def swap(value, at, second):
    axes = ("gx", "gy", "gz")
    sizes = [lax.axis_size(axis) for axis in axes]
    other = 0 if at == 2 else 2
    pairs = []
    for index in np.ndindex(*sizes):
        target = list(index)
        if not second:
            target[at] ^= 1
        elif 0 < index[at] < sizes[at] - 1:
            target[at] = ((index[at] - 1) ^ 1) + 1
        else:
            target[other] ^= 1
        pairs.append(tuple(int(np.ravel_multi_index(i, sizes)) for i in (index, target)))
    return lax.ppermute(value, axes, pairs)


def body(displ, veloc, accel, node_index, inv_map, jac_weight, lame_first, shear_mod, density):
    f32 = functools.partial(jax.ShapeDtypeStruct, dtype=F32)
    flat = (3, 1, NODES)
    points = (125, 1, 128)
    tables = [jnp.asarray(table) for table in operator_tables()]
    scratch = [
        pltpu.VMEM(flat, F32), pltpu.VMEM(flat, F32), pltpu.VMEM(flat, F32),
        pltpu.VMEM((1, 1, 128), jnp.int32),
        pltpu.VMEM((9, 128, 128), F32),
        pltpu.VMEM((128, 128), F32), pltpu.VMEM((128, 128), F32),
        pltpu.VMEM((128, 128), F32), pltpu.VMEM((128, 128), F32),
        pltpu.VMEM((768, 128), BF16), pltpu.VMEM((256, 384), BF16),
        pltpu.VMEM(flat, F32), pltpu.VMEM((3, 24, 640), F32), pltpu.VMEM((3, 9, 24, 128), F32),
        pltpu.VMEM((3, 128, 128), F32), pltpu.VMEM((384, 384), F32),
        pltpu.VMEM((384, 384), BF16), pltpu.VMEM((384, 384), BF16),
        pltpu.SemaphoreType.DMA((20,)),
    ]
    terms, slots, ya, v_half, displ_out = pl.pallas_call(
        force_kernel,
        out_shape=(
            f32((4, 200, 128)), jax.ShapeDtypeStruct((8, 128), jnp.int32), f32((XPAD, 128)),
            f32(flat), f32(flat),
        ),
        in_specs=[HBM] * 11,
        out_specs=(VMEM, VMEM, VMEM, VMEM, HBM),
        scratch_shapes=scratch,
        compiler_params=pltpu.CompilerParams(vmem_limit_bytes=16 << 20),
    )(
        *(
            pltpu.with_memory_space_constraint(value, pltpu.HBM)
            for value in (
                displ.reshape(flat), veloc.reshape(flat), accel.reshape(flat),
                node_index.reshape(points), inv_map.reshape(1125, 1, 128),
                jac_weight.reshape(points), lame_first.reshape(points), shear_mod.reshape(points),
                density.reshape(points), *tables,
            )
        )
    )
    small = pltpu.CompilerParams(vmem_limit_bytes=8 << 20)
    ya = swap(ya, 1, False)
    field = pl.pallas_call(
        field_kernel,
        out_shape=f32((FROWS, 128)),
        in_specs=[VMEM] * 2,
        out_specs=VMEM,
        compiler_params=small,
        cost_estimate=pl.CostEstimate(flops=4000000, bytes_accessed=800000, transcendentals=0),
    )(terms, slots)
    count = lax.axis_size("gy")
    hops = [(i, (i + 2) % count if i % 2 == 0 else (i - 2) % count) for i in range(count)]
    yb = lax.ppermute(ya, "gy", hops)
    face = f32((40, 128))
    xa, xb = pl.pallas_call(
        x_kernel,
        out_shape=(face, face),
        in_specs=[VMEM] * 3,
        out_specs=(VMEM,) * 2,
        compiler_params=small,
    )(ya, yb, field)
    field = pl.pallas_call(
        y_kernel,
        out_shape=f32((FROWS, 128)),
        in_specs=[VMEM] * 3,
        out_specs=VMEM,
        input_output_aliases={2: 0},
        compiler_params=small,
        cost_estimate=pl.CostEstimate(flops=1000000, bytes_accessed=800000, transcendentals=0),
    )(ya, yb, field)
    xa = swap(xa, 0, False)
    xb = swap(xb, 0, True)
    face = f32((96, 128))
    field, za, zb = pl.pallas_call(
        z_kernel,
        out_shape=(f32((FROWS, 128)), face, face),
        in_specs=[VMEM] * 3,
        out_specs=(VMEM,) * 3,
        input_output_aliases={2: 0},
        compiler_params=pltpu.CompilerParams(vmem_limit_bytes=8 << 20),
    )(xa, xb, field)
    za = swap(za, 2, False)
    zb = swap(zb, 2, True)
    veloc_out, accel_out = pl.pallas_call(
        end_kernel,
        out_shape=(f32(flat), f32(flat)),
        in_specs=[VMEM] * 4,
        out_specs=(HBM, HBM),
        scratch_shapes=[
            pltpu.VMEM(flat, F32), pltpu.VMEM(flat, F32), pltpu.VMEM((3, 9, 24, 128), F32),
            pltpu.VMEM((3, 24, 640), F32), pltpu.SemaphoreType.DMA((2,)),
        ],
        compiler_params=pltpu.CompilerParams(vmem_limit_bytes=8 << 20),
    )(za, zb, field, v_half)
    shape = (3, 1, 1, 1, NODES)
    return displ_out.reshape(shape), veloc_out.reshape(shape), accel_out.reshape(shape)


def solution(mesh):
    nodal = P(None, "gx", "gy", "gz", None)
    point = P("gx", "gy", "gz", None, None)
    placed = (nodal,) * 3 + (point, P("gx", "gy", "gz", None, None, None)) + (point,) * 4
    return jax.shard_map(
        body, mesh=mesh, in_specs=placed, out_specs=(nodal,) * 3, check_vma=False
    )
```

time: 169 us -> 30.5 us (0.18)
  local copies, waits for them, and re-layouts: 113 us -> 0 us
  matrix products: 8.97 us -> 0 us
  Pallas kernels: 0 us -> 8.51 us
  waiting for transfers between devices: 13.5 us -> 5.14 us
  other arithmetic: 8.09 us -> 0 us
  starting transfers between devices: 23.1 us -> 16.1 us
    transpose x27 -> x0, local copies, waits for them, and re-layouts: 42.3 us -> none  [the longest x12 21 us: fold_points(): lead = jnp.moveaxis(lead, axis, axis + 1)]
    slice x30 -> x0, local copies, waits for them, and re-layouts: 34.7 us -> none  [the longest x5 27.4 us: split_points(): lax.slice_in_dim(grid, offset, offset + 4 * (count - 1) + 1, stride=4, ax...]
    another operation x11 -> x0, local copies, waits for them, and re-layouts: 15 us -> none  [the longest x2 9.54 us: element_terms(): local = local.reshape(3, 5, 5, 5, elements)]
    dot_general x6 -> x0, matrix products: 8.97 us -> none  [the longest x1 6.76 us: element_terms(): jnp.einsum('kp,cabpe->cabke', deriv, local, precision=highest)]
    pallas_call x0 -> x6, Pallas kernels: none -> 8.51 us  [the longest x1 4.46 us: body(): pl.pallas_call(force_kernel, out_shape=(f32((4, 200, 128)), jax.ShapeDtyp...]
    ppermute x6, waiting for transfers between devices: 13.5 us -> 5.14 us  [the longest x5 4.45 us: swap(): return lax.ppermute(value, axes, pairs)]
    ppermute x6, starting transfers between devices: 23.1 us -> 16.1 us  [the longest x5 14.8 us: swap(): return lax.ppermute(value, axes, pairs)]
    unnamed x71 -> x0, local copies, waits for them, and re-layouts: 6.38 us -> none
  transfers between devices with their start and end apart: 6 -> 6, of which waited for: 3 -> 5; matrix products, arithmetic and copies ran while one was open for 1% -> 0% of each run, Pallas kernels for 0% -> 8%
where the time goes in v1:
time: 30.5 us; the launch traced here: 30.4 us
  starting transfers between devices  16.1 us (53%)
  Pallas kernels  8.51 us (28%)
  waiting for transfers between devices  5.14 us (17%)
  between operations  0.67 us (2%)
    ppermute x5, starting transfers between devices, swap(): return lax.ppermute(value, axes, pairs)  14.8 us
    pallas_call x1, Pallas kernels, body(): pl.pallas_call(force_kernel, out_shape=(f32((4, 200, 128)), jax.ShapeDtyp...  4.46 us
    ppermute x5, waiting for transfers between devices, swap(): return lax.ppermute(value, axes, pairs)  4.45 us
    pallas_call x1, Pallas kernels, body(): pl.pallas_call(field_kernel, out_shape=f32((FROWS, 128)), in_specs=[VMEM]...  1.83 us
    pallas_call x1, Pallas kernels, body(): pl.pallas_call(end_kernel, out_shape=(f32(flat), f32(flat)), in_specs=[VM...  1.45 us
    ppermute x1, starting transfers between devices, body(): yb = lax.ppermute(ya, 'gy', hops)  1.3 us
    ppermute x1, waiting for transfers between devices, body(): yb = lax.ppermute(ya, 'gy', hops)  0.69 us
  transfers between devices with their start and end apart: 6, of which 5 were waited for; matrix products, arithmetic and copies ran while one was open for 0% of the time, Pallas kernels for 8%

profile of v1, /device:TPU:1, one launch (start us, length us, event | category | flops | bytes accessed | tf_op | source)
XLA Modules:
  0.0 30.4 jit_solution(7422179408844156227)
XLA Ops:
  0.6 4.5 %shard_map.130 = (f32[4,200,128]{2,1,0:T(8,128)S(1)}, s32[8,128]{1,0:T(8,128)S(1)}, f32[24,128]{1,0:T(8,128)S(1)}, f32[3,1,9945]{2,1,0:T(1,128)S(1)}, f32[3,1,9945]{2,1,0:T(1,128)}) custom-call(f32[3,1,9945]{2,1,0:T(1,128)} %bitcast.19, f32[3,1,9945]{2,1,0:T(1,128)} %bitcast.20, f32[3,1,9945]{2,1,0:T(1,128)} %bitcast.21, s32[125,1,128]{2,1,0:T(1,128)} %bitcast.22, ...), custom_call_target="tpu_custom_call" | custom-call | tf_op jit(solution)/shard_map/pallas_call | solution.py:437
  5.1 7.8 %collective-permute-start = (f32[24,128]{1,0:T(8,128)S(1)}, f32[24,128]{1,0:T(8,128)S(1)}, u32[]{:S(2)}, u32[]{:S(2)}) collective-permute-start(f32[24,128]{1,0:T(8,128)S(1)} %get-tuple-element.16), channel_id=1, source_target_pairs={{0,8},{1,9},{2,10},{3,11},{4,12},{5,13},{6,14},{7,15},{8,0},{9,1},... | collective-permute-start | bytes 36872 | tf_op jit(solution)/shard_map/ppermute | solution.py:417
  12.9 1.1 %collective-permute-done.ya_ref = f32[24,128]{1,0:T(8,128)S(1)} collective-permute-done((f32[24,128]{1,0:T(8,128)S(1)}, f32[24,128]{1,0:T(8,128)S(1)}, u32[]{:S(2)}, u32[]{:S(2)}) %collective-permute-start) | collective-permute-done | bytes 12320 | tf_op jit(solution)/shard_map/ppermute | solution.py:417
  14.0 1.3 %collective-permute-start.1 = (f32[24,128]{1,0:T(8,128)S(1)}, f32[24,128]{1,0:T(8,128)S(1)}, u32[]{:S(2)}, u32[]{:S(2)}) collective-permute-start(f32[24,128]{1,0:T(8,128)S(1)} %collective-permute-done.ya_ref), channel_id=1, source_target_pairs={{0,16},{8,56},{16,32},{24,8},{32,48},{40,24},{48,0},{56,40},{1,17}... | collective-permute-start | bytes 36872 | tf_op jit(solution)/shard_map/ppermute | solution.py:470
  15.3 1.8 %shard_map.131.f_ref.f_in = f32[960,128]{1,0:T(8,128)S(1)} custom-call(f32[4,200,128]{2,1,0:T(8,128)S(1)} %get-tuple-element.17.t_ref, s32[8,128]{1,0:T(8,128)S(1)} %get-tuple-element.18.o_ref), custom_call_target="tpu_custom_call" | custom-call | flops 4000000 | bytes 800000 | tf_op jit(solution)/shard_map/pallas_call | solution.py:460
  17.1 0.7 %collective-permute-done.1.yb_ref = f32[24,128]{1,0:T(8,128)S(1)} collective-permute-done((f32[24,128]{1,0:T(8,128)S(1)}, f32[24,128]{1,0:T(8,128)S(1)}, u32[]{:S(2)}, u32[]{:S(2)}) %collective-permute-start.1) | collective-permute-done | bytes 12320 | tf_op jit(solution)/shard_map/ppermute | solution.py:470
  17.8 0.2 shard_map.132
  18.0 0.8 %collective-permute-start.2 = (f32[40,128]{1,0:T(8,128)S(1)}, f32[40,128]{1,0:T(8,128)S(1)}, u32[]{:S(2)}, u32[]{:S(2)}) collective-permute-start(f32[40,128]{1,0:T(8,128)S(1)} %get-tuple-element.19), channel_id=1, source_target_pairs={{0,64},{1,65},{2,66},{3,67},{4,68},{5,69},{6,70},{7,71},{8,72},{9,... | collective-permute-start | bytes 61448 | tf_op jit(solution)/shard_map/ppermute | solution.py:417
  18.8 2.9 %collective-permute-start.3 = (f32[40,128]{1,0:T(8,128)S(1)}, f32[40,128]{1,0:T(8,128)S(1)}, u32[]{:S(2)}, u32[]{:S(2)}) collective-permute-start(f32[40,128]{1,0:T(8,128)S(1)} %get-tuple-element.20), channel_id=1, source_target_pairs={{0,1},{1,0},{2,3},{3,2},{4,5},{5,4},{6,7},{7,6},{8,9},{9,8},{10,11... | collective-permute-start | bytes 61448 | tf_op jit(solution)/shard_map/ppermute | solution.py:417
  21.7 0.5 %shard_map.133.f_in = f32[960,128]{1,0:T(8,128)S(1)} custom-call(f32[24,128]{1,0:T(8,128)S(1)} %collective-permute-done.ya_ref, f32[24,128]{1,0:T(8,128)S(1)} %collective-permute-done.1.yb_ref, f32[960,128]{1,0:T(8,128)S(1)} %shard_map.131.f_ref.f_in), custom_call_target="tpu_custom_call", output_to_operand_aliasing={{}: (2, {})} | custom-call | flops 1000000 | bytes 800000 | tf_op jit(solution)/shard_map/pallas_call | solution.py:479
  22.3 0.0 collective-permute-done.2.xa_ref
  22.3 0.3 %collective-permute-done.3.xb_ref = f32[40,128]{1,0:T(8,128)S(1)} collective-permute-done((f32[40,128]{1,0:T(8,128)S(1)}, f32[40,128]{1,0:T(8,128)S(1)}, u32[]{:S(2)}, u32[]{:S(2)}) %collective-permute-start.3) | collective-permute-done | bytes 20512 | tf_op jit(solution)/shard_map/ppermute | solution.py:417
  22.6 0.1 shard_map.134
  22.7 2.5 %collective-permute-start.4 = (f32[96,128]{1,0:T(8,128)S(1)}, f32[96,128]{1,0:T(8,128)S(1)}, u32[]{:S(2)}, u32[]{:S(2)}) collective-permute-start(f32[96,128]{1,0:T(8,128)S(1)} %get-tuple-element.21), channel_id=1, source_target_pairs={{0,1},{1,0},{2,3},{3,2},{4,5},{5,4},{6,7},{7,6},{8,9},{9,8},{10,11... | collective-permute-start | bytes 147464 | tf_op jit(solution)/shard_map/ppermute | solution.py:417
  25.1 0.8 %collective-permute-start.5 = (f32[96,128]{1,0:T(8,128)S(1)}, f32[96,128]{1,0:T(8,128)S(1)}, u32[]{:S(2)}, u32[]{:S(2)}) collective-permute-start(f32[96,128]{1,0:T(8,128)S(1)} %get-tuple-element.22), channel_id=1, source_target_pairs={{0,64},{1,2},{2,1},{3,4},{4,3},{5,6},{6,5},{7,71},{8,72},{9,10},{1... | collective-permute-start | bytes 147464 | tf_op jit(solution)/shard_map/ppermute | solution.py:417
  25.9 0.1 collective-permute-done.4.za_ref
  26.0 2.9 %collective-permute-done.5.zb_ref = f32[96,128]{1,0:T(8,128)S(1)} collective-permute-done((f32[96,128]{1,0:T(8,128)S(1)}, f32[96,128]{1,0:T(8,128)S(1)}, u32[]{:S(2)}, u32[]{:S(2)}) %collective-permute-start.5) | collective-permute-done | bytes 49184 | tf_op jit(solution)/shard_map/ppermute | solution.py:417
  28.9 1.4 %shard_map.135 = (f32[3,1,9945]{2,1,0:T(1,128)}, f32[3,1,9945]{2,1,0:T(1,128)}) custom-call(f32[96,128]{1,0:T(8,128)S(1)} %collective-permute-done.4.za_ref, f32[96,128]{1,0:T(8,128)S(1)} %collective-permute-done.5.zb_ref, f32[960,128]{1,0:T(8,128)S(1)} %get-tuple-element.23.f_ref, f32[3,1,9945]{2,1,0:T(1,128)S(1)} %get-tuple-element.24.vh_ref), custom_call_target="tpu_custom_call" | custom-call | tf_op jit(solution)/shard_map/pallas_call | solution.py:501
Async XLA Ops:
  5.1 8.9 %collective-permute-start = (f32[24,128]{1,0:T(8,128)S(1)}, f32[24,128]{1,0:T(8,128)S(1)}, u32[]{:S(2)}, u32[]{:S(2)}) collective-permute-start(f32[24,128]{1,0:T(8,128)S(1)} %get-tuple-element.16), channel_id=1, source_target_pairs={{0,8},{1,9},{2,10},{3,11},{4,12},{5,13},{6,14},{7,15},{8,0},{9,1},... | collective-permute-start | bytes 36872 | tf_op jit(solution)/shard_map/ppermute | solution.py:417
  14.0 3.8 %collective-permute-start.1 = (f32[24,128]{1,0:T(8,128)S(1)}, f32[24,128]{1,0:T(8,128)S(1)}, u32[]{:S(2)}, u32[]{:S(2)}) collective-permute-start(f32[24,128]{1,0:T(8,128)S(1)} %collective-permute-done.ya_ref), channel_id=1, source_target_pairs={{0,16},{8,56},{16,32},{24,8},{32,48},{40,24},{48,0},{56,40},{1,17}... | collective-permute-start | bytes 36872 | tf_op jit(solution)/shard_map/ppermute | solution.py:470
  18.0 4.3 %collective-permute-start.2 = (f32[40,128]{1,0:T(8,128)S(1)}, f32[40,128]{1,0:T(8,128)S(1)}, u32[]{:S(2)}, u32[]{:S(2)}) collective-permute-start(f32[40,128]{1,0:T(8,128)S(1)} %get-tuple-element.19), channel_id=1, source_target_pairs={{0,64},{1,65},{2,66},{3,67},{4,68},{5,69},{6,70},{7,71},{8,72},{9,... | collective-permute-start | bytes 61448 | tf_op jit(solution)/shard_map/ppermute | solution.py:417
  18.8 3.8 %collective-permute-start.3 = (f32[40,128]{1,0:T(8,128)S(1)}, f32[40,128]{1,0:T(8,128)S(1)}, u32[]{:S(2)}, u32[]{:S(2)}) collective-permute-start(f32[40,128]{1,0:T(8,128)S(1)} %get-tuple-element.20), channel_id=1, source_target_pairs={{0,1},{1,0},{2,3},{3,2},{4,5},{5,4},{6,7},{7,6},{8,9},{9,8},{10,11... | collective-permute-start | bytes 61448 | tf_op jit(solution)/shard_map/ppermute | solution.py:417
  22.7 3.3 %collective-permute-start.4 = (f32[96,128]{1,0:T(8,128)S(1)}, f32[96,128]{1,0:T(8,128)S(1)}, u32[]{:S(2)}, u32[]{:S(2)}) collective-permute-start(f32[96,128]{1,0:T(8,128)S(1)} %get-tuple-element.21), channel_id=1, source_target_pairs={{0,1},{1,0},{2,3},{3,2},{4,5},{5,4},{6,7},{7,6},{8,9},{9,8},{10,11... | collective-permute-start | bytes 147464 | tf_op jit(solution)/shard_map/ppermute | solution.py:417
  25.1 3.8 %collective-permute-start.5 = (f32[96,128]{1,0:T(8,128)S(1)}, f32[96,128]{1,0:T(8,128)S(1)}, u32[]{:S(2)}, u32[]{:S(2)}) collective-permute-start(f32[96,128]{1,0:T(8,128)S(1)} %get-tuple-element.22), channel_id=1, source_target_pairs={{0,64},{1,2},{2,1},{3,4},{4,3},{5,6},{6,5},{7,71},{8,72},{9,10},{1... | collective-permute-start | bytes 147464 | tf_op jit(solution)/shard_map/ppermute | solution.py:417

commit v2 on v1

--- a/solution.py
+++ b/solution.py
@@ -128,31 +128,44 @@
 
     for m in range(3):
         for x in range(NX):
-            grid_s[m, x : x + 1, :ROW] = pos_s[m, :, pl.ds(ROW * x, ROW)]
-    for m in range(3):
-        for tile in range(3):
-            parts = [grid_s[m, 8 * tile : 8 * tile + 8, 128 * v : 128 * v + 128] for v in range(5)]
-            for z in range(NZ):
-                at = 9 * lane + z
-                low = at & 127
-                high = at >> 7
+            value = pos_s[m, :, pl.ds(ROW * x, ROW)]
+            if x < 16:
+                grid_s[m, x : x + 1, :ROW] = value
+            else:
+                grid_s[3, m : m + 1, :ROW] = value
+    places = [9 * (lane & 63) + 4 * (lane >> 6) + c for c in range(5)]
+    for u in range(2):
+        c = jnp.minimum(4 * u + (lane >> 5), 4)
+        places.append(36 * (lane & 15) + 36 + c + 4 * ((lane >> 4) & 1))
+    for m in range(4):
+        for tile in range(2 if m < 3 else 1):
+            rows = slice(8 * tile, 8 * tile + 8)
+            parts = [grid_s[m, rows, 128 * v : 128 * v + 128] for v in range(5)]
+            for c in range(7):
+                low = places[c] & 127
+                high = places[c] >> 7
                 got = take(parts[0], low)
                 for v in range(1, 5):
                     got = jnp.where(high == v, take(parts[v], low), got)
-                nodal_s[m, z, 8 * tile : 8 * tile + 8, :] = got
-
-    masks = [group == g for g in range(8)]
-    indices = [4 * elem_y + b for b in range(5)]
+                if m < 3:
+                    nodal_s[m, c, rows, :] = got
+                else:
+                    for k in range(3):
+                        nodal_s[k, c, 16:17, :] = got[k : k + 1]
+
+    masks = [elem_x == x for x in range(4)]
+    inner = 64 * elem_z + 4 * elem_y
+    outer = 16 * elem_z + elem_y
     for m in range(3):
         local_s[m, 120:128, :] = jnp.zeros((8, 128), F32)
         for c in range(5):
-            parts = [
-                nodal_s[m, 4 * (g % 2) + c, 4 * (g // 2) : 4 * (g // 2) + 8, :] for g in range(8)
-            ]
+            near = [nodal_s[m, c, 4 * x : 4 * x + 8, :] for x in range(4)]
+            last = [nodal_s[m, 5 + c // 4, 4 * x : 4 * x + 8, :] for x in range(4)]
             for b in range(5):
-                got = take(parts[0], indices[b])
-                for g in range(1, 8):
-                    got = jnp.where(masks[g], take(parts[g], indices[b]), got)
+                parts, at = (near, inner + b) if b < 4 else (last, outer + 32 * (c % 4))
+                got = take(parts[0], at)
+                for x in range(1, 4):
+                    got = jnp.where(masks[x], take(parts[x], at), got)
                 local_s[m, pl.ds(5 * b + c, 5, stride=25), :] = got[:5]
 
     copies[4].wait()
@@ -362,6 +375,11 @@
     odd = at % 2 == 1
     outer = (at > 0) & (at < lax.axis_size("gz") - 1)
     lane = lanes()
+    spots = []
+    for v in range(5):
+        at = lane + 128 * v
+        y = jnp.floor((at.astype(F32) + 0.5) * (1.0 / 9.0)).astype(jnp.int32)
+        spots.append((y, at - 9 * y))
 
     def added(m, z, tile):
         value = f_ref[(m * 9 + z) * XPAD + 8 * tile : (m * 9 + z) * XPAD + 8 * tile + 8, :]
@@ -372,32 +390,40 @@
             value = value + (jnp.where(odd, near, far) if z == 0 else jnp.where(odd, far, near))
         return value
 
+    def to_rows(m, tile):
+        rows = slice(8 * tile, 8 * tile + 8)
+        parts = [acc_s[m, z, rows, :] for z in range(NZ)]
+        for v in range(5):
+            y, z_of = spots[v]
+            got = take(parts[0], y)
+            for z in range(1, NZ):
+                got = jnp.where(z_of == z, take(parts[z], y), got)
+            grid_s[m, rows, 128 * v : 128 * v + 128] = got
+
     for z in range(NZ):
         for tile in range(3):
             mass = added(3, z, tile)
             for m in range(3):
-                acc_s[m, z, 8 * tile : 8 * tile + 8, :] = added(m, z, tile) / mass
+                value = added(m, z, tile) / mass
+                if tile < 2:
+                    acc_s[m, z, 8 * tile : 8 * tile + 8, :] = value
+                else:
+                    acc_s[3, z, m : m + 1, :] = value[0:1]
+    to_rows(3, 0)
+    copies = []
     for m in range(3):
-        for tile in range(3):
-            parts = [acc_s[m, z, 8 * tile : 8 * tile + 8, :] for z in range(NZ)]
-            for v in range(5):
-                at = lane + 128 * v
-                y = jnp.floor((at.astype(F32) + 0.5) * (1.0 / 9.0)).astype(jnp.int32)
-                z_of = at - 9 * y
-                got = take(parts[0], y)
-                for z in range(1, NZ):
-                    got = jnp.where(z_of == z, take(parts[z], y), got)
-                grid_s[m, 8 * tile : 8 * tile + 8, 128 * v : 128 * v + 128] = got
-    for m in range(3):
-        for x in range(NX):
+        to_rows(m, 0)
+        to_rows(m, 1)
+        for x in range(16):
             a_s[m, :, pl.ds(ROW * x, ROW)] = grid_s[m, x : x + 1, :ROW]
-    a_copy = pltpu.make_async_copy(a_s, a_out, sems.at[0])
-    a_copy.start()
-    v_s[...] = vh_ref[...] + HALF * a_s[...]
-    v_copy = pltpu.make_async_copy(v_s, v_out, sems.at[1])
-    v_copy.start()
-    a_copy.wait()
-    v_copy.wait()
+        a_s[m, :, pl.ds(ROW * 16, ROW)] = grid_s[3, m : m + 1, :ROW]
+        v_s[m] = vh_ref[m] + HALF * a_s[m]
+        for k, (src, dst) in enumerate(((a_s, a_out), (v_s, v_out))):
+            copy = pltpu.make_async_copy(src.at[m], dst.at[m], sems.at[2 * m + k])
+            copy.start()
+            copies.append(copy)
+    for copy in copies:
+        copy.wait()
 
 
 def swap(value, at, second):
@@ -429,7 +455,7 @@
         pltpu.VMEM((128, 128), F32), pltpu.VMEM((128, 128), F32),
         pltpu.VMEM((128, 128), F32), pltpu.VMEM((128, 128), F32),
         pltpu.VMEM((768, 128), BF16), pltpu.VMEM((256, 384), BF16),
-        pltpu.VMEM(flat, F32), pltpu.VMEM((3, 24, 640), F32), pltpu.VMEM((3, 9, 24, 128), F32),
+        pltpu.VMEM(flat, F32), pltpu.VMEM((4, 16, 640), F32), pltpu.VMEM((3, 7, 24, 128), F32),
         pltpu.VMEM((3, 128, 128), F32), pltpu.VMEM((384, 384), F32),
         pltpu.VMEM((384, 384), BF16), pltpu.VMEM((384, 384), BF16),
         pltpu.SemaphoreType.DMA((20,)),
@@ -504,8 +530,8 @@
         in_specs=[VMEM] * 4,
         out_specs=(HBM, HBM),
         scratch_shapes=[
-            pltpu.VMEM(flat, F32), pltpu.VMEM(flat, F32), pltpu.VMEM((3, 9, 24, 128), F32),
-            pltpu.VMEM((3, 24, 640), F32), pltpu.SemaphoreType.DMA((2,)),
+            pltpu.VMEM(flat, F32), pltpu.VMEM(flat, F32), pltpu.VMEM((4, 9, 16, 128), F32),
+            pltpu.VMEM((4, 16, 640), F32), pltpu.SemaphoreType.DMA((6,)),
         ],
         compiler_params=pltpu.CompilerParams(vmem_limit_bytes=8 << 20),
     )(za, zb, field, v_half)

time: 30.5 us -> 30 us (0.984)
  Pallas kernels: 8.51 us -> 8.01 us
    pallas_call x1, Pallas kernels: 4.46 us -> 3.87 us  [body(): pl.pallas_call(force_kernel, out_shape=(f32((4, 200, 128)), jax.ShapeDtyp...]
where the time goes in v2:
time: 30 us; the launch traced here: 29.9 us
  starting transfers between devices  16.1 us (54%)
  Pallas kernels  8.01 us (27%)
  waiting for transfers between devices  5.14 us (17%)
  between operations  0.67 us (2%)
    ppermute x5, starting transfers between devices, swap(): return lax.ppermute(value, axes, pairs)  14.8 us
    ppermute x5, waiting for transfers between devices, swap(): return lax.ppermute(value, axes, pairs)  4.45 us
    pallas_call x1, Pallas kernels, body(): pl.pallas_call(force_kernel, out_shape=(f32((4, 200, 128)), jax.ShapeDtyp...  3.87 us
    pallas_call x1, Pallas kernels, body(): pl.pallas_call(field_kernel, out_shape=f32((FROWS, 128)), in_specs=[VMEM]...  1.83 us
    pallas_call x1, Pallas kernels, body(): pl.pallas_call(end_kernel, out_shape=(f32(flat), f32(flat)), in_specs=[VM...  1.53 us
    ppermute x1, starting transfers between devices, body(): yb = lax.ppermute(ya, 'gy', hops)  1.3 us
    ppermute x1, waiting for transfers between devices, body(): yb = lax.ppermute(ya, 'gy', hops)  0.69 us
  transfers between devices with their start and end apart: 6, of which 5 were waited for; matrix products, arithmetic and copies ran while one was open for 0% of the time, Pallas kernels for 8%

profile of v2, /device:TPU:1, one launch (start us, length us, event | category | flops | bytes accessed | tf_op | source)
XLA Modules:
  0.0 29.9 jit_solution(13736757856769851794)
XLA Ops:
  0.6 3.9 %shard_map.130 = (f32[4,200,128]{2,1,0:T(8,128)S(1)}, s32[8,128]{1,0:T(8,128)S(1)}, f32[24,128]{1,0:T(8,128)S(1)}, f32[3,1,9945]{2,1,0:T(1,128)S(1)}, f32[3,1,9945]{2,1,0:T(1,128)}) custom-call(f32[3,1,9945]{2,1,0:T(1,128)} %bitcast.19, f32[3,1,9945]{2,1,0:T(1,128)} %bitcast.20, f32[3,1,9945]{2,1,0:T(1,128)} %bitcast.21, s32[125,1,128]{2,1,0:T(1,128)} %bitcast.22, ...), custom_call_target="tpu_custom_call" | custom-call | tf_op jit(solution)/shard_map/pallas_call | solution.py:463
  4.5 7.8 %collective-permute-start = (f32[24,128]{1,0:T(8,128)S(1)}, f32[24,128]{1,0:T(8,128)S(1)}, u32[]{:S(2)}, u32[]{:S(2)}) collective-permute-start(f32[24,128]{1,0:T(8,128)S(1)} %get-tuple-element.16), channel_id=1, source_target_pairs={{0,8},{1,9},{2,10},{3,11},{4,12},{5,13},{6,14},{7,15},{8,0},{9,1},... | collective-permute-start | bytes 36872 | tf_op jit(solution)/shard_map/ppermute | solution.py:443
  12.3 1.1 %collective-permute-done.ya_ref = f32[24,128]{1,0:T(8,128)S(1)} collective-permute-done((f32[24,128]{1,0:T(8,128)S(1)}, f32[24,128]{1,0:T(8,128)S(1)}, u32[]{:S(2)}, u32[]{:S(2)}) %collective-permute-start) | collective-permute-done | bytes 12320 | tf_op jit(solution)/shard_map/ppermute | solution.py:443
  13.4 1.3 %collective-permute-start.1 = (f32[24,128]{1,0:T(8,128)S(1)}, f32[24,128]{1,0:T(8,128)S(1)}, u32[]{:S(2)}, u32[]{:S(2)}) collective-permute-start(f32[24,128]{1,0:T(8,128)S(1)} %collective-permute-done.ya_ref), channel_id=1, source_target_pairs={{0,16},{8,56},{16,32},{24,8},{32,48},{40,24},{48,0},{56,40},{1,17}... | collective-permute-start | bytes 36872 | tf_op jit(solution)/shard_map/ppermute | solution.py:496
  14.7 1.8 %shard_map.131.f_ref.f_in = f32[960,128]{1,0:T(8,128)S(1)} custom-call(f32[4,200,128]{2,1,0:T(8,128)S(1)} %get-tuple-element.17.t_ref, s32[8,128]{1,0:T(8,128)S(1)} %get-tuple-element.18.o_ref), custom_call_target="tpu_custom_call" | custom-call | flops 4000000 | bytes 800000 | tf_op jit(solution)/shard_map/pallas_call | solution.py:486
  16.5 0.7 %collective-permute-done.1.yb_ref = f32[24,128]{1,0:T(8,128)S(1)} collective-permute-done((f32[24,128]{1,0:T(8,128)S(1)}, f32[24,128]{1,0:T(8,128)S(1)}, u32[]{:S(2)}, u32[]{:S(2)}) %collective-permute-start.1) | collective-permute-done | bytes 12320 | tf_op jit(solution)/shard_map/ppermute | solution.py:496
  17.2 0.2 shard_map.132
  17.4 0.8 %collective-permute-start.2 = (f32[40,128]{1,0:T(8,128)S(1)}, f32[40,128]{1,0:T(8,128)S(1)}, u32[]{:S(2)}, u32[]{:S(2)}) collective-permute-start(f32[40,128]{1,0:T(8,128)S(1)} %get-tuple-element.19), channel_id=1, source_target_pairs={{0,64},{1,65},{2,66},{3,67},{4,68},{5,69},{6,70},{7,71},{8,72},{9,... | collective-permute-start | bytes 61448 | tf_op jit(solution)/shard_map/ppermute | solution.py:443
  18.2 2.9 %collective-permute-start.3 = (f32[40,128]{1,0:T(8,128)S(1)}, f32[40,128]{1,0:T(8,128)S(1)}, u32[]{:S(2)}, u32[]{:S(2)}) collective-permute-start(f32[40,128]{1,0:T(8,128)S(1)} %get-tuple-element.20), channel_id=1, source_target_pairs={{0,1},{1,0},{2,3},{3,2},{4,5},{5,4},{6,7},{7,6},{8,9},{9,8},{10,11... | collective-permute-start | bytes 61448 | tf_op jit(solution)/shard_map/ppermute | solution.py:443
  21.2 0.5 %shard_map.133.f_in = f32[960,128]{1,0:T(8,128)S(1)} custom-call(f32[24,128]{1,0:T(8,128)S(1)} %collective-permute-done.ya_ref, f32[24,128]{1,0:T(8,128)S(1)} %collective-permute-done.1.yb_ref, f32[960,128]{1,0:T(8,128)S(1)} %shard_map.131.f_ref.f_in), custom_call_target="tpu_custom_call", output_to_operand_aliasing={{}: (2, {})} | custom-call | flops 1000000 | bytes 800000 | tf_op jit(solution)/shard_map/pallas_call | solution.py:505
  21.7 0.0 collective-permute-done.2.xa_ref
  21.7 0.3 %collective-permute-done.3.xb_ref = f32[40,128]{1,0:T(8,128)S(1)} collective-permute-done((f32[40,128]{1,0:T(8,128)S(1)}, f32[40,128]{1,0:T(8,128)S(1)}, u32[]{:S(2)}, u32[]{:S(2)}) %collective-permute-start.3) | collective-permute-done | bytes 20512 | tf_op jit(solution)/shard_map/ppermute | solution.py:443
  22.0 0.1 shard_map.134
  22.1 2.5 %collective-permute-start.4 = (f32[96,128]{1,0:T(8,128)S(1)}, f32[96,128]{1,0:T(8,128)S(1)}, u32[]{:S(2)}, u32[]{:S(2)}) collective-permute-start(f32[96,128]{1,0:T(8,128)S(1)} %get-tuple-element.21), channel_id=1, source_target_pairs={{0,1},{1,0},{2,3},{3,2},{4,5},{5,4},{6,7},{7,6},{8,9},{9,8},{10,11... | collective-permute-start | bytes 147464 | tf_op jit(solution)/shard_map/ppermute | solution.py:443
  24.5 0.7 %collective-permute-start.5 = (f32[96,128]{1,0:T(8,128)S(1)}, f32[96,128]{1,0:T(8,128)S(1)}, u32[]{:S(2)}, u32[]{:S(2)}) collective-permute-start(f32[96,128]{1,0:T(8,128)S(1)} %get-tuple-element.22), channel_id=1, source_target_pairs={{0,64},{1,2},{2,1},{3,4},{4,3},{5,6},{6,5},{7,71},{8,72},{9,10},{1... | collective-permute-start | bytes 147464 | tf_op jit(solution)/shard_map/ppermute | solution.py:443
  25.3 0.1 collective-permute-done.4.za_ref
  25.4 2.9 %collective-permute-done.5.zb_ref = f32[96,128]{1,0:T(8,128)S(1)} collective-permute-done((f32[96,128]{1,0:T(8,128)S(1)}, f32[96,128]{1,0:T(8,128)S(1)}, u32[]{:S(2)}, u32[]{:S(2)}) %collective-permute-start.5) | collective-permute-done | bytes 49184 | tf_op jit(solution)/shard_map/ppermute | solution.py:443
  28.3 1.5 %shard_map.135 = (f32[3,1,9945]{2,1,0:T(1,128)}, f32[3,1,9945]{2,1,0:T(1,128)}) custom-call(f32[96,128]{1,0:T(8,128)S(1)} %collective-permute-done.4.za_ref, f32[96,128]{1,0:T(8,128)S(1)} %collective-permute-done.5.zb_ref, f32[960,128]{1,0:T(8,128)S(1)} %get-tuple-element.23.f_ref, f32[3,1,9945]{2,1,0:T(1,128)S(1)} %get-tuple-element.24.vh_ref), custom_call_target="tpu_custom_call" | custom-call | tf_op jit(solution)/shard_map/pallas_call | solution.py:527
Async XLA Ops:
  4.5 8.9 %collective-permute-start = (f32[24,128]{1,0:T(8,128)S(1)}, f32[24,128]{1,0:T(8,128)S(1)}, u32[]{:S(2)}, u32[]{:S(2)}) collective-permute-start(f32[24,128]{1,0:T(8,128)S(1)} %get-tuple-element.16), channel_id=1, source_target_pairs={{0,8},{1,9},{2,10},{3,11},{4,12},{5,13},{6,14},{7,15},{8,0},{9,1},... | collective-permute-start | bytes 36872 | tf_op jit(solution)/shard_map/ppermute | solution.py:443
  13.4 3.8 %collective-permute-start.1 = (f32[24,128]{1,0:T(8,128)S(1)}, f32[24,128]{1,0:T(8,128)S(1)}, u32[]{:S(2)}, u32[]{:S(2)}) collective-permute-start(f32[24,128]{1,0:T(8,128)S(1)} %collective-permute-done.ya_ref), channel_id=1, source_target_pairs={{0,16},{8,56},{16,32},{24,8},{32,48},{40,24},{48,0},{56,40},{1,17}... | collective-permute-start | bytes 36872 | tf_op jit(solution)/shard_map/ppermute | solution.py:496
  17.4 4.3 %collective-permute-start.2 = (f32[40,128]{1,0:T(8,128)S(1)}, f32[40,128]{1,0:T(8,128)S(1)}, u32[]{:S(2)}, u32[]{:S(2)}) collective-permute-start(f32[40,128]{1,0:T(8,128)S(1)} %get-tuple-element.19), channel_id=1, source_target_pairs={{0,64},{1,65},{2,66},{3,67},{4,68},{5,69},{6,70},{7,71},{8,72},{9,... | collective-permute-start | bytes 61448 | tf_op jit(solution)/shard_map/ppermute | solution.py:443
  18.2 3.8 %collective-permute-start.3 = (f32[40,128]{1,0:T(8,128)S(1)}, f32[40,128]{1,0:T(8,128)S(1)}, u32[]{:S(2)}, u32[]{:S(2)}) collective-permute-start(f32[40,128]{1,0:T(8,128)S(1)} %get-tuple-element.20), channel_id=1, source_target_pairs={{0,1},{1,0},{2,3},{3,2},{4,5},{5,4},{6,7},{7,6},{8,9},{9,8},{10,11... | collective-permute-start | bytes 61448 | tf_op jit(solution)/shard_map/ppermute | solution.py:443
  22.1 3.3 %collective-permute-start.4 = (f32[96,128]{1,0:T(8,128)S(1)}, f32[96,128]{1,0:T(8,128)S(1)}, u32[]{:S(2)}, u32[]{:S(2)}) collective-permute-start(f32[96,128]{1,0:T(8,128)S(1)} %get-tuple-element.21), channel_id=1, source_target_pairs={{0,1},{1,0},{2,3},{3,2},{4,5},{5,4},{6,7},{7,6},{8,9},{9,8},{10,11... | collective-permute-start | bytes 147464 | tf_op jit(solution)/shard_map/ppermute | solution.py:443
  24.5 3.8 %collective-permute-start.5 = (f32[96,128]{1,0:T(8,128)S(1)}, f32[96,128]{1,0:T(8,128)S(1)}, u32[]{:S(2)}, u32[]{:S(2)}) collective-permute-start(f32[96,128]{1,0:T(8,128)S(1)} %get-tuple-element.22), channel_id=1, source_target_pairs={{0,64},{1,2},{2,1},{3,4},{4,3},{5,6},{6,5},{7,71},{8,72},{9,10},{1... | collective-permute-start | bytes 147464 | tf_op jit(solution)/shard_map/ppermute | solution.py:443

commit v3 on v2

--- a/solution.py
+++ b/solution.py
@@ -84,9 +84,9 @@
 
 def force_kernel(
     d_hbm, v_hbm, a_hbm, n_hbm, m_hbm, j_hbm, l_hbm, s_hbm, r_hbm, fw_hbm, bw_hbm,
-    t_ref, o_ref, y_ref, vh_ref, d_out,
+    t_ref, o_ref, y_ref, vh_ref, pos_s,
     d_s, v_s, a_s, n_s, m_s, j_s, l_s, s_s, r_s, fw_s, bw_s,
-    pos_s, grid_s, nodal_s, local_s, grad_s, fluxh_s, fluxl_s, sems,
+    grid_s, nodal_s, local_s, grad_s, fluxh_s, fluxl_s, sems,
 ):
     copies = []
     moves = [(d_hbm, d_s), (v_hbm, v_s), (a_hbm, a_s), (n_hbm.at[pl.ds(0, 1)], n_s), (fw_hbm, fw_s)]
@@ -105,8 +105,6 @@
     veloc = v_s[...]
     pos_s[...] = d_s[...] + time_step * veloc + HALF_SQ * accel
     vh_ref[...] = veloc + HALF * accel
-    out_copy = pltpu.make_async_copy(pos_s, d_out, sems.at[19])
-    out_copy.start()
     lane = lanes()
 
     corner = jnp.broadcast_to(n_s[0], (8, 128))
@@ -259,7 +257,6 @@
                 total = total + jnp.where(good & ((k >> 3) == q), take(packs[q], at), zero)
         parts.append(total)
     stack_rows(parts, row, zero, y_ref, 0)
-    out_copy.wait()
 
 
 def stack_rows(parts, row, zero, out_ref, at):
@@ -272,7 +269,9 @@
     out_ref[at + 16 : at + 24, :] = jnp.where(row < 4, fourth, zero)
 
 
-def field_kernel(t_ref, o_ref, f_ref):
+def field_kernel(t_ref, o_ref, d_ref, f_ref, d_out, sem):
+    out_copy = pltpu.make_async_copy(d_ref, d_out, sem)
+    out_copy.start()
     slot_of = o_ref[...]
     lane = lanes()
     gathers = []
@@ -302,6 +301,7 @@
         for z in range(NZ):
             stack_rows([planes[(z, x)] for x in range(4)], row, zero, f_ref, (m * 9 + z) * XPAD)
     f_ref[36 * XPAD : FROWS, :] = jnp.zeros((FROWS - 36 * XPAD, 128), F32)
+    out_copy.wait()
 
 
 def y_faces(ya, yb):
@@ -370,60 +370,88 @@
         zb_ref[XPAD * m : XPAD * m + XPAD, :] = jnp.where(odd, last, first)
 
 
-def end_kernel(za_ref, zb_ref, f_ref, vh_ref, v_out, a_out, a_s, v_s, acc_s, grid_s, sems):
-    at = lax.axis_index("gz")
-    odd = at % 2 == 1
-    outer = (at > 0) & (at < lax.axis_size("gz") - 1)
-    lane = lanes()
+def row_spots(lane):
     spots = []
     for v in range(5):
         at = lane + 128 * v
         y = jnp.floor((at.astype(F32) + 0.5) * (1.0 / 9.0)).astype(jnp.int32)
         spots.append((y, at - 9 * y))
+    return spots
+
+
+def inner_kernel(f_ref, grid_ref, acc_s):
+    for z in range(1, 8):
+        for tile in range(3):
+            rows = [(m * 9 + z) * XPAD + 8 * tile for m in range(4)]
+            mass = f_ref[rows[3] : rows[3] + 8, :]
+            for m in range(3):
+                value = f_ref[rows[m] : rows[m] + 8, :] / mass
+                if tile < 2:
+                    acc_s[m, z, 8 * tile : 8 * tile + 8, :] = value
+                else:
+                    acc_s[3, z, m : m + 1, :] = value[0:1]
+    spots = row_spots(lanes())
+    for m in range(4):
+        for tile in range(2 if m < 3 else 1):
+            rows = slice(8 * tile, 8 * tile + 8)
+            for v in range(5):
+                y, z_of = spots[v]
+                got = take(acc_s[m, 1, rows, :], y)
+                for z in range(2, 8):
+                    got = jnp.where(z_of == z, take(acc_s[m, z, rows, :], y), got)
+                grid_ref[m, rows, 128 * v : 128 * v + 128] = got
+    grid_ref[3, 8:16, :] = jnp.zeros((8, 640), F32)
+
+
+def end_kernel(
+    za_ref, zb_ref, f_ref, vh_ref, inner_ref, v_out, a_out, a_s, v_s, acc_s, grid_s, sems
+):
+    at = lax.axis_index("gz")
+    odd = at % 2 == 1
+    outer = (at > 0) & (at < lax.axis_size("gz") - 1)
+    spots = row_spots(lanes())
 
     def added(m, z, tile):
-        value = f_ref[(m * 9 + z) * XPAD + 8 * tile : (m * 9 + z) * XPAD + 8 * tile + 8, :]
-        if z in (0, 8):
-            rows = slice(XPAD * m + 8 * tile, XPAD * m + 8 * tile + 8)
-            near = za_ref[rows, :]
-            far = jnp.where(outer, zb_ref[rows, :], 0.0)
-            value = value + (jnp.where(odd, near, far) if z == 0 else jnp.where(odd, far, near))
-        return value
+        at = (m * 9 + z) * XPAD + 8 * tile
+        rows = slice(XPAD * m + 8 * tile, XPAD * m + 8 * tile + 8)
+        near = za_ref[rows, :]
+        far = jnp.where(outer, zb_ref[rows, :], 0.0)
+        return f_ref[at : at + 8, :] + (
+            jnp.where(odd, near, far) if z == 0 else jnp.where(odd, far, near)
+        )
 
     def to_rows(m, tile):
         rows = slice(8 * tile, 8 * tile + 8)
-        parts = [acc_s[m, z, rows, :] for z in range(NZ)]
         for v in range(5):
             y, z_of = spots[v]
-            got = take(parts[0], y)
-            for z in range(1, NZ):
-                got = jnp.where(z_of == z, take(parts[z], y), got)
-            grid_s[m, rows, 128 * v : 128 * v + 128] = got
-
-    for z in range(NZ):
+            cols = slice(128 * v, 128 * v + 128)
+            got = jnp.where(z_of == 0, take(acc_s[m, 0, rows, :], y), inner_ref[m, rows, cols])
+            got = jnp.where(z_of == 8, take(acc_s[m, 1, rows, :], y), got)
+            grid_s[m, rows, cols] = got
+
+    for z in (0, 8):
         for tile in range(3):
             mass = added(3, z, tile)
             for m in range(3):
                 value = added(m, z, tile) / mass
                 if tile < 2:
-                    acc_s[m, z, 8 * tile : 8 * tile + 8, :] = value
+                    acc_s[m, z // 8, 8 * tile : 8 * tile + 8, :] = value
                 else:
-                    acc_s[3, z, m : m + 1, :] = value[0:1]
+                    acc_s[3, z // 8, m : m + 1, :] = value[0:1]
     to_rows(3, 0)
-    copies = []
     for m in range(3):
         to_rows(m, 0)
         to_rows(m, 1)
         for x in range(16):
             a_s[m, :, pl.ds(ROW * x, ROW)] = grid_s[m, x : x + 1, :ROW]
         a_s[m, :, pl.ds(ROW * 16, ROW)] = grid_s[3, m : m + 1, :ROW]
-        v_s[m] = vh_ref[m] + HALF * a_s[m]
-        for k, (src, dst) in enumerate(((a_s, a_out), (v_s, v_out))):
-            copy = pltpu.make_async_copy(src.at[m], dst.at[m], sems.at[2 * m + k])
-            copy.start()
-            copies.append(copy)
-    for copy in copies:
-        copy.wait()
+    a_copy = pltpu.make_async_copy(a_s, a_out, sems.at[0])
+    a_copy.start()
+    v_s[...] = vh_ref[...] + HALF * a_s[...]
+    v_copy = pltpu.make_async_copy(v_s, v_out, sems.at[1])
+    v_copy.start()
+    a_copy.wait()
+    v_copy.wait()
 
 
 def swap(value, at, second):
@@ -455,19 +483,19 @@
         pltpu.VMEM((128, 128), F32), pltpu.VMEM((128, 128), F32),
         pltpu.VMEM((128, 128), F32), pltpu.VMEM((128, 128), F32),
         pltpu.VMEM((768, 128), BF16), pltpu.VMEM((256, 384), BF16),
-        pltpu.VMEM(flat, F32), pltpu.VMEM((4, 16, 640), F32), pltpu.VMEM((3, 7, 24, 128), F32),
+        pltpu.VMEM((4, 16, 640), F32), pltpu.VMEM((3, 7, 24, 128), F32),
         pltpu.VMEM((3, 128, 128), F32), pltpu.VMEM((384, 384), F32),
         pltpu.VMEM((384, 384), BF16), pltpu.VMEM((384, 384), BF16),
-        pltpu.SemaphoreType.DMA((20,)),
+        pltpu.SemaphoreType.DMA((19,)),
     ]
-    terms, slots, ya, v_half, displ_out = pl.pallas_call(
+    terms, slots, ya, v_half, displ_new = pl.pallas_call(
         force_kernel,
         out_shape=(
             f32((4, 200, 128)), jax.ShapeDtypeStruct((8, 128), jnp.int32), f32((XPAD, 128)),
             f32(flat), f32(flat),
         ),
         in_specs=[HBM] * 11,
-        out_specs=(VMEM, VMEM, VMEM, VMEM, HBM),
+        out_specs=(VMEM,) * 5,
         scratch_shapes=scratch,
         compiler_params=pltpu.CompilerParams(vmem_limit_bytes=16 << 20),
     )(
@@ -483,14 +511,15 @@
     )
     small = pltpu.CompilerParams(vmem_limit_bytes=8 << 20)
     ya = swap(ya, 1, False)
-    field = pl.pallas_call(
+    field, displ_out = pl.pallas_call(
         field_kernel,
-        out_shape=f32((FROWS, 128)),
-        in_specs=[VMEM] * 2,
-        out_specs=VMEM,
+        out_shape=(f32((FROWS, 128)), f32(flat)),
+        in_specs=[VMEM] * 3,
+        out_specs=(VMEM, HBM),
+        scratch_shapes=[pltpu.SemaphoreType.DMA],
         compiler_params=small,
         cost_estimate=pl.CostEstimate(flops=4000000, bytes_accessed=800000, transcendentals=0),
-    )(terms, slots)
+    )(terms, slots, displ_new)
     count = lax.axis_size("gy")
     hops = [(i, (i + 2) % count if i % 2 == 0 else (i - 2) % count) for i in range(count)]
     yb = lax.ppermute(ya, "gy", hops)
@@ -524,17 +553,26 @@
     )(xa, xb, field)
     za = swap(za, 2, False)
     zb = swap(zb, 2, True)
+    inner = pl.pallas_call(
+        inner_kernel,
+        out_shape=f32((4, 16, 640)),
+        in_specs=[VMEM],
+        out_specs=VMEM,
+        scratch_shapes=[pltpu.VMEM((4, 9, 16, 128), F32)],
+        compiler_params=small,
+        cost_estimate=pl.CostEstimate(flops=1000000, bytes_accessed=800000, transcendentals=0),
+    )(field)
     veloc_out, accel_out = pl.pallas_call(
         end_kernel,
         out_shape=(f32(flat), f32(flat)),
-        in_specs=[VMEM] * 4,
+        in_specs=[VMEM] * 5,
         out_specs=(HBM, HBM),
         scratch_shapes=[
-            pltpu.VMEM(flat, F32), pltpu.VMEM(flat, F32), pltpu.VMEM((4, 9, 16, 128), F32),
-            pltpu.VMEM((4, 16, 640), F32), pltpu.SemaphoreType.DMA((6,)),
+            pltpu.VMEM(flat, F32), pltpu.VMEM(flat, F32), pltpu.VMEM((4, 2, 16, 128), F32),
+            pltpu.VMEM((4, 16, 640), F32), pltpu.SemaphoreType.DMA((2,)),
         ],
         compiler_params=pltpu.CompilerParams(vmem_limit_bytes=8 << 20),
-    )(za, zb, field, v_half)
+    )(za, zb, field, v_half, inner)
     shape = (3, 1, 1, 1, NODES)
     return displ_out.reshape(shape), veloc_out.reshape(shape), accel_out.reshape(shape)
 

time: 30 us -> 29.5 us (0.983)
  waiting for transfers between devices: 5.14 us -> 4.13 us
  Pallas kernels: 8.01 us -> 8.57 us
    pallas_call x1 -> x2, Pallas kernels: 1.83 us -> 2.83 us  [the longest x1 2.37 us: body(): pl.pallas_call(field_kernel, out_shape=(f32((FROWS, 128)), f32(flat)), in...]
    ppermute x1, waiting for transfers between devices: 0.69 us -> 0.14 us  [body(): yb = lax.ppermute(ya, 'gy', hops)]
    ppermute x5, waiting for transfers between devices: 4.45 us -> 3.99 us  [swap(): return lax.ppermute(value, axes, pairs)]
    pallas_call x1, Pallas kernels: 1.53 us -> 1.1 us  [body(): pl.pallas_call(end_kernel, out_shape=(f32(flat), f32(flat)), in_specs=[VM...]
  transfers between devices with their start and end apart: 6 -> 6, of which waited for: 5 -> 4; matrix products, arithmetic and copies ran while one was open for 0% -> 0% of each run, Pallas kernels for 8% -> 11%
where the time goes in v3:
time: 29.5 us; the launch traced here: 29.4 us
  starting transfers between devices  16.1 us (55%)
  Pallas kernels  8.57 us (29%)
  waiting for transfers between devices  4.13 us (14%)
  between operations  0.68 us (2%)
    ppermute x5, starting transfers between devices, swap(): return lax.ppermute(value, axes, pairs)  14.8 us
    ppermute x5, waiting for transfers between devices, swap(): return lax.ppermute(value, axes, pairs)  3.99 us
    pallas_call x1, Pallas kernels, body(): pl.pallas_call(force_kernel, out_shape=(f32((4, 200, 128)), jax.ShapeDtyp...  3.87 us
    pallas_call x1, Pallas kernels, body(): pl.pallas_call(field_kernel, out_shape=(f32((FROWS, 128)), f32(flat)), in...  2.37 us
    ppermute x1, starting transfers between devices, body(): yb = lax.ppermute(ya, 'gy', hops)  1.3 us
    pallas_call x1, Pallas kernels, body(): pl.pallas_call(end_kernel, out_shape=(f32(flat), f32(flat)), in_specs=[VM...  1.1 us
  transfers between devices with their start and end apart: 6, of which 4 were waited for; matrix products, arithmetic and copies ran while one was open for 0% of the time, Pallas kernels for 11%

profile of v3, /device:TPU:1, one launch (start us, length us, event | category | flops | bytes accessed | tf_op | source)
XLA Modules:
  0.0 29.4 jit_solution(11506023122284985395)
XLA Ops:
  0.6 3.9 %shard_map.130 = (f32[4,200,128]{2,1,0:T(8,128)S(1)}, s32[8,128]{1,0:T(8,128)S(1)}, f32[24,128]{1,0:T(8,128)S(1)}, f32[3,1,9945]{2,1,0:T(1,128)S(1)}, f32[3,1,9945]{2,1,0:T(1,128)S(1)}) custom-call(f32[3,1,9945]{2,1,0:T(1,128)} %bitcast.19, f32[3,1,9945]{2,1,0:T(1,128)} %bitcast.20, f32[3,1,9945]{2,1,0:T(1,128)} %bitcast.21, s32[125,1,128]{2,1,0:T(1,128)} %bitcast.22, ...), custom_call_target="tpu_custom_call" | custom-call | tf_op jit(solution)/shard_map/pallas_call | solution.py:491
  4.5 7.8 %collective-permute-start = (f32[24,128]{1,0:T(8,128)S(1)}, f32[24,128]{1,0:T(8,128)S(1)}, u32[]{:S(2)}, u32[]{:S(2)}) collective-permute-start(f32[24,128]{1,0:T(8,128)S(1)} %get-tuple-element.21), channel_id=1, source_target_pairs={{0,8},{1,9},{2,10},{3,11},{4,12},{5,13},{6,14},{7,15},{8,0},{9,1},... | collective-permute-start | bytes 36872 | tf_op jit(solution)/shard_map/ppermute | solution.py:471
  12.3 1.1 %collective-permute-done.ya_ref = f32[24,128]{1,0:T(8,128)S(1)} collective-permute-done((f32[24,128]{1,0:T(8,128)S(1)}, f32[24,128]{1,0:T(8,128)S(1)}, u32[]{:S(2)}, u32[]{:S(2)}) %collective-permute-start) | collective-permute-done | bytes 12320 | tf_op jit(solution)/shard_map/ppermute | solution.py:471
  13.4 1.3 %collective-permute-start.1 = (f32[24,128]{1,0:T(8,128)S(1)}, f32[24,128]{1,0:T(8,128)S(1)}, u32[]{:S(2)}, u32[]{:S(2)}) collective-permute-start(f32[24,128]{1,0:T(8,128)S(1)} %collective-permute-done.ya_ref), channel_id=1, source_target_pairs={{0,16},{8,56},{16,32},{24,8},{32,48},{40,24},{48,0},{56,40},{1,17}... | collective-permute-start | bytes 36872 | tf_op jit(solution)/shard_map/ppermute | solution.py:525
  14.7 2.4 %shard_map.131 = (f32[960,128]{1,0:T(8,128)S(1)}, f32[3,1,9945]{2,1,0:T(1,128)}) custom-call(f32[4,200,128]{2,1,0:T(8,128)S(1)} %get-tuple-element.17.t_ref, s32[8,128]{1,0:T(8,128)S(1)} %get-tuple-element.18.o_ref, f32[3,1,9945]{2,1,0:T(1,128)S(1)} %get-tuple-element.19.d_ref), custom_call_target="tpu_custom_call" | custom-call | flops 4000000 | bytes 800000 | tf_op jit(solution)/shard_map/pallas_call | solution.py:514
  17.1 0.1 collective-permute-done.1.yb_ref
  17.2 0.2 shard_map.132
  17.4 0.8 %collective-permute-start.2 = (f32[40,128]{1,0:T(8,128)S(1)}, f32[40,128]{1,0:T(8,128)S(1)}, u32[]{:S(2)}, u32[]{:S(2)}) collective-permute-start(f32[40,128]{1,0:T(8,128)S(1)} %get-tuple-element.23), channel_id=1, source_target_pairs={{0,64},{1,65},{2,66},{3,67},{4,68},{5,69},{6,70},{7,71},{8,72},{9,... | collective-permute-start | bytes 61448 | tf_op jit(solution)/shard_map/ppermute | solution.py:471
  18.2 2.9 %collective-permute-start.3 = (f32[40,128]{1,0:T(8,128)S(1)}, f32[40,128]{1,0:T(8,128)S(1)}, u32[]{:S(2)}, u32[]{:S(2)}) collective-permute-start(f32[40,128]{1,0:T(8,128)S(1)} %get-tuple-element.24), channel_id=1, source_target_pairs={{0,1},{1,0},{2,3},{3,2},{4,5},{5,4},{6,7},{7,6},{8,9},{9,8},{10,11... | collective-permute-start | bytes 61448 | tf_op jit(solution)/shard_map/ppermute | solution.py:471
  21.1 0.5 %shard_map.133.f_in = f32[960,128]{1,0:T(8,128)S(1)} custom-call(f32[24,128]{1,0:T(8,128)S(1)} %collective-permute-done.ya_ref, f32[24,128]{1,0:T(8,128)S(1)} %collective-permute-done.1.yb_ref, f32[960,128]{1,0:T(8,128)S(1)} %get-tuple-element.22.f_ref.f_in), custom_call_target="tpu_custom_call", output_to_operand_aliasing={{}: (2, {})} | custom-call | flops 1000000 | bytes 800000 | tf_op jit(solution)/shard_map/pallas_call | solution.py:534
  21.7 0.0 collective-permute-done.2.xa_ref
  21.7 0.3 %collective-permute-done.3.xb_ref = f32[40,128]{1,0:T(8,128)S(1)} collective-permute-done((f32[40,128]{1,0:T(8,128)S(1)}, f32[40,128]{1,0:T(8,128)S(1)}, u32[]{:S(2)}, u32[]{:S(2)}) %collective-permute-start.3) | collective-permute-done | bytes 20512 | tf_op jit(solution)/shard_map/ppermute | solution.py:471
  22.0 0.1 shard_map.134
  22.1 2.5 %collective-permute-start.4 = (f32[96,128]{1,0:T(8,128)S(1)}, f32[96,128]{1,0:T(8,128)S(1)}, u32[]{:S(2)}, u32[]{:S(2)}) collective-permute-start(f32[96,128]{1,0:T(8,128)S(1)} %get-tuple-element.25), channel_id=1, source_target_pairs={{0,1},{1,0},{2,3},{3,2},{4,5},{5,4},{6,7},{7,6},{8,9},{9,8},{10,11... | collective-permute-start | bytes 147464 | tf_op jit(solution)/shard_map/ppermute | solution.py:471
  24.5 0.7 %collective-permute-start.5 = (f32[96,128]{1,0:T(8,128)S(1)}, f32[96,128]{1,0:T(8,128)S(1)}, u32[]{:S(2)}, u32[]{:S(2)}) collective-permute-start(f32[96,128]{1,0:T(8,128)S(1)} %get-tuple-element.26), channel_id=1, source_target_pairs={{0,64},{1,2},{2,1},{3,4},{4,3},{5,6},{6,5},{7,71},{8,72},{9,10},{1... | collective-permute-start | bytes 147464 | tf_op jit(solution)/shard_map/ppermute | solution.py:471
  25.3 0.5 %shard_map.135.inner_ref = f32[4,16,640]{2,1,0:T(8,128)S(1)} custom-call(f32[960,128]{1,0:T(8,128)S(1)} %get-tuple-element.27.f_ref), custom_call_target="tpu_custom_call" | custom-call | flops 1000000 | bytes 800000 | tf_op jit(solution)/shard_map/pallas_call | solution.py:556
  25.7 0.0 collective-permute-done.4.za_ref
  25.8 2.6 %collective-permute-done.5.zb_ref = f32[96,128]{1,0:T(8,128)S(1)} collective-permute-done((f32[96,128]{1,0:T(8,128)S(1)}, f32[96,128]{1,0:T(8,128)S(1)}, u32[]{:S(2)}, u32[]{:S(2)}) %collective-permute-start.5) | collective-permute-done | bytes 49184 | tf_op jit(solution)/shard_map/ppermute | solution.py:471
  28.3 1.1 %shard_map.136 = (f32[3,1,9945]{2,1,0:T(1,128)}, f32[3,1,9945]{2,1,0:T(1,128)}) custom-call(f32[96,128]{1,0:T(8,128)S(1)} %collective-permute-done.4.za_ref, f32[96,128]{1,0:T(8,128)S(1)} %collective-permute-done.5.zb_ref, f32[960,128]{1,0:T(8,128)S(1)} %get-tuple-element.27.f_ref, f32[3,1,9945]{2,1,0:T(1,128)S(1)} %get-tuple-element.28.vh_ref, ...), custom_call_target="tpu_custom_call" | custom-call | tf_op jit(solution)/shard_map/pallas_call | solution.py:565
Async XLA Ops:
  4.5 8.9 %collective-permute-start = (f32[24,128]{1,0:T(8,128)S(1)}, f32[24,128]{1,0:T(8,128)S(1)}, u32[]{:S(2)}, u32[]{:S(2)}) collective-permute-start(f32[24,128]{1,0:T(8,128)S(1)} %get-tuple-element.21), channel_id=1, source_target_pairs={{0,8},{1,9},{2,10},{3,11},{4,12},{5,13},{6,14},{7,15},{8,0},{9,1},... | collective-permute-start | bytes 36872 | tf_op jit(solution)/shard_map/ppermute | solution.py:471
  13.4 3.8 %collective-permute-start.1 = (f32[24,128]{1,0:T(8,128)S(1)}, f32[24,128]{1,0:T(8,128)S(1)}, u32[]{:S(2)}, u32[]{:S(2)}) collective-permute-start(f32[24,128]{1,0:T(8,128)S(1)} %collective-permute-done.ya_ref), channel_id=1, source_target_pairs={{0,16},{8,56},{16,32},{24,8},{32,48},{40,24},{48,0},{56,40},{1,17}... | collective-permute-start | bytes 36872 | tf_op jit(solution)/shard_map/ppermute | solution.py:525
  17.4 4.3 %collective-permute-start.2 = (f32[40,128]{1,0:T(8,128)S(1)}, f32[40,128]{1,0:T(8,128)S(1)}, u32[]{:S(2)}, u32[]{:S(2)}) collective-permute-start(f32[40,128]{1,0:T(8,128)S(1)} %get-tuple-element.23), channel_id=1, source_target_pairs={{0,64},{1,65},{2,66},{3,67},{4,68},{5,69},{6,70},{7,71},{8,72},{9,... | collective-permute-start | bytes 61448 | tf_op jit(solution)/shard_map/ppermute | solution.py:471
  18.2 3.8 %collective-permute-start.3 = (f32[40,128]{1,0:T(8,128)S(1)}, f32[40,128]{1,0:T(8,128)S(1)}, u32[]{:S(2)}, u32[]{:S(2)}) collective-permute-start(f32[40,128]{1,0:T(8,128)S(1)} %get-tuple-element.24), channel_id=1, source_target_pairs={{0,1},{1,0},{2,3},{3,2},{4,5},{5,4},{6,7},{7,6},{8,9},{9,8},{10,11... | collective-permute-start | bytes 61448 | tf_op jit(solution)/shard_map/ppermute | solution.py:471
  22.1 3.7 %collective-permute-start.4 = (f32[96,128]{1,0:T(8,128)S(1)}, f32[96,128]{1,0:T(8,128)S(1)}, u32[]{:S(2)}, u32[]{:S(2)}) collective-permute-start(f32[96,128]{1,0:T(8,128)S(1)} %get-tuple-element.25), channel_id=1, source_target_pairs={{0,1},{1,0},{2,3},{3,2},{4,5},{5,4},{6,7},{7,6},{8,9},{9,8},{10,11... | collective-permute-start | bytes 147464 | tf_op jit(solution)/shard_map/ppermute | solution.py:471
  24.5 3.8 %collective-permute-start.5 = (f32[96,128]{1,0:T(8,128)S(1)}, f32[96,128]{1,0:T(8,128)S(1)}, u32[]{:S(2)}, u32[]{:S(2)}) collective-permute-start(f32[96,128]{1,0:T(8,128)S(1)} %get-tuple-element.26), channel_id=1, source_target_pairs={{0,64},{1,2},{2,1},{3,4},{4,3},{5,6},{6,5},{7,71},{8,72},{9,10},{1... | collective-permute-start | bytes 147464 | tf_op jit(solution)/shard_map/ppermute | solution.py:471

commit v4 on v3

--- a/solution.py
+++ b/solution.py
@@ -61,8 +61,12 @@
     for matrix in (forward, backward):
         high = matrix.astype(np.float32).astype(jnp.bfloat16)
         low = (matrix - high.astype(np.float64)).astype(np.float32).astype(jnp.bfloat16)
-        out.append(np.concatenate([high, low], axis=0))
-    return out
+        out.append((high, low))
+    (forward_h, forward_l), (backward_h, backward_l) = out
+    return (
+        np.concatenate([forward_h, forward_l, forward_h], axis=1),
+        np.concatenate([backward_h, backward_l], axis=0),
+    )
 
 
 def split(value):
@@ -89,7 +93,10 @@
     grid_s, nodal_s, local_s, grad_s, fluxh_s, fluxl_s, sems,
 ):
     copies = []
-    moves = [(d_hbm, d_s), (v_hbm, v_s), (a_hbm, a_s), (n_hbm.at[pl.ds(0, 1)], n_s), (fw_hbm, fw_s)]
+    moves = [(n_hbm.at[pl.ds(0, 1)], n_s)]
+    for src, dst in ((d_hbm, d_s), (v_hbm, v_s), (a_hbm, a_s)):
+        moves += [(src.at[m], dst.at[m]) for m in range(3)]
+    moves.append((fw_hbm, fw_s))
     for k in range(9):
         moves.append((m_hbm.at[pl.ds(125 * k, 125), 0], m_s.at[k, pl.ds(0, 125)]))
     for src, dst in ((j_hbm, j_s), (l_hbm, l_s), (s_hbm, s_s), (r_hbm, r_s)):
@@ -99,7 +106,7 @@
         copy = pltpu.make_async_copy(src, dst, sems.at[at])
         copy.start()
         copies.append(copy)
-    for at in range(4):
+    for at in range(10):
         copies[at].wait()
     accel = a_s[...]
     veloc = v_s[...]
@@ -166,13 +173,12 @@
                     got = jnp.where(masks[x], take(parts[x], at), got)
                 local_s[m, pl.ds(5 * b + c, 5, stride=25), :] = got[:5]
 
-    copies[4].wait()
+    copies[10].wait()
     local = jnp.concatenate([local_s[m] for m in range(3)], axis=1)
     high, low = split(local)
-    both = dot(fw_s[...], high)
-    grad_s[...] = both[:384] + both[384:] + dot(fw_s[0:384, :], low)
-
-    for at in range(5, 18):
+    grad_s[...] = dot(fw_s[...], jnp.concatenate([high, high, low], axis=0))
+
+    for at in range(11, 24):
         copies[at].wait()
     for chunk in range(8):
         at = 16 * chunk
@@ -210,7 +216,7 @@
                 fluxh_s[to, cols] = high
                 fluxl_s[to, cols] = low
 
-    copies[18].wait()
+    copies[24].wait()
     both = dot(bw_s[...], fluxh_s[...])
     terms = both[:128] + both[128:] + dot(bw_s[0:128, :], fluxl_s[...])
     for m in range(3):
@@ -269,9 +275,7 @@
     out_ref[at + 16 : at + 24, :] = jnp.where(row < 4, fourth, zero)
 
 
-def field_kernel(t_ref, o_ref, d_ref, f_ref, d_out, sem):
-    out_copy = pltpu.make_async_copy(d_ref, d_out, sem)
-    out_copy.start()
+def field_kernel(t_ref, o_ref, f_ref):
     slot_of = o_ref[...]
     lane = lanes()
     gathers = []
@@ -301,22 +305,20 @@
         for z in range(NZ):
             stack_rows([planes[(z, x)] for x in range(4)], row, zero, f_ref, (m * 9 + z) * XPAD)
     f_ref[36 * XPAD : FROWS, :] = jnp.zeros((FROWS - 36 * XPAD, 128), F32)
-    out_copy.wait()
-
-
-def y_faces(ya, yb):
+
+
+def y_faces(near, far):
     at = lax.axis_index("gy")
     odd = at % 2 == 1
     outer = (at > 0) & (at < lax.axis_size("gy") - 1)
-    far = jnp.where(outer, yb, 0.0)
-    return jnp.where(odd, ya, far), jnp.where(odd, far, ya)
-
-
-def x_kernel(ya_ref, yb_ref, f_ref, xa_ref, xb_ref):
+    far = jnp.where(outer, far, 0.0)
+    return jnp.where(odd, near, far), jnp.where(odd, far, near)
+
+
+def x_kernel(y_ref, f_ref, xa_ref, xb_ref):
     pad = jnp.zeros((128 - XPAD, 128), F32)
-    near = jnp.concatenate([ya_ref[...], pad], axis=0).T[0:40]
-    far = jnp.concatenate([yb_ref[...], pad], axis=0).T[64:104]
-    lo, hi = y_faces(near, far)
+    both = jnp.concatenate([y_ref[...], pad], axis=0).T
+    lo, hi = y_faces(both[0:40], both[64:104])
     lane = lanes((40, 128))
 
     def face(x):
@@ -333,11 +335,11 @@
     xb_ref[...] = jnp.where(odd, last, first)
 
 
-def y_kernel(ya_ref, yb_ref, f_in, f_ref):
+def y_kernel(y_ref, f_in, f_ref):
     lane = lanes()
     for tile in range(3):
         rows = slice(8 * tile, 8 * tile + 8)
-        lo, hi = y_faces(ya_ref[rows, :], pltpu.roll(yb_ref[rows, :], 64, 1))
+        lo, hi = y_faces(y_ref[rows, :], pltpu.roll(y_ref[rows, :], 64, 1))
         for plane in range(36):
             to = slice(plane * XPAD + 8 * tile, plane * XPAD + 8 * tile + 8)
             low = pltpu.roll(lo, 128 - plane, 1) if plane else lo
@@ -379,7 +381,9 @@
     return spots
 
 
-def inner_kernel(f_ref, grid_ref, acc_s):
+def inner_kernel(f_ref, d_ref, grid_ref, d_out, acc_s, sem):
+    out_copy = pltpu.make_async_copy(d_ref, d_out, sem)
+    out_copy.start()
     for z in range(1, 8):
         for tile in range(3):
             rows = [(m * 9 + z) * XPAD + 8 * tile for m in range(4)]
@@ -401,6 +405,7 @@
                     got = jnp.where(z_of == z, take(acc_s[m, z, rows, :], y), got)
                 grid_ref[m, rows, 128 * v : 128 * v + 128] = got
     grid_ref[3, 8:16, :] = jnp.zeros((8, 640), F32)
+    out_copy.wait()
 
 
 def end_kernel(
@@ -482,11 +487,11 @@
         pltpu.VMEM((9, 128, 128), F32),
         pltpu.VMEM((128, 128), F32), pltpu.VMEM((128, 128), F32),
         pltpu.VMEM((128, 128), F32), pltpu.VMEM((128, 128), F32),
-        pltpu.VMEM((768, 128), BF16), pltpu.VMEM((256, 384), BF16),
+        pltpu.VMEM((384, 384), BF16), pltpu.VMEM((256, 384), BF16),
         pltpu.VMEM((4, 16, 640), F32), pltpu.VMEM((3, 7, 24, 128), F32),
         pltpu.VMEM((3, 128, 128), F32), pltpu.VMEM((384, 384), F32),
         pltpu.VMEM((384, 384), BF16), pltpu.VMEM((384, 384), BF16),
-        pltpu.SemaphoreType.DMA((19,)),
+        pltpu.SemaphoreType.DMA((25,)),
     ]
     terms, slots, ya, v_half, displ_new = pl.pallas_call(
         force_kernel,
@@ -510,36 +515,35 @@
         )
     )
     small = pltpu.CompilerParams(vmem_limit_bytes=8 << 20)
-    ya = swap(ya, 1, False)
-    field, displ_out = pl.pallas_call(
+    count = lax.axis_size("gy")
+    hops = [(i, (i - 2) % count if i % 2 == 0 else (i + 2) % count) for i in range(count)]
+    passed = lax.ppermute(ya, "gy", hops)
+    ya = swap(jnp.where(lanes((XPAD, 128)) < 64, ya, passed), 1, False)
+    field = pl.pallas_call(
         field_kernel,
-        out_shape=(f32((FROWS, 128)), f32(flat)),
-        in_specs=[VMEM] * 3,
-        out_specs=(VMEM, HBM),
-        scratch_shapes=[pltpu.SemaphoreType.DMA],
+        out_shape=f32((FROWS, 128)),
+        in_specs=[VMEM] * 2,
+        out_specs=VMEM,
         compiler_params=small,
         cost_estimate=pl.CostEstimate(flops=4000000, bytes_accessed=800000, transcendentals=0),
-    )(terms, slots, displ_new)
-    count = lax.axis_size("gy")
-    hops = [(i, (i + 2) % count if i % 2 == 0 else (i - 2) % count) for i in range(count)]
-    yb = lax.ppermute(ya, "gy", hops)
+    )(terms, slots)
     face = f32((40, 128))
     xa, xb = pl.pallas_call(
         x_kernel,
         out_shape=(face, face),
-        in_specs=[VMEM] * 3,
+        in_specs=[VMEM] * 2,
         out_specs=(VMEM,) * 2,
         compiler_params=small,
-    )(ya, yb, field)
+    )(ya, field)
     field = pl.pallas_call(
         y_kernel,
         out_shape=f32((FROWS, 128)),
-        in_specs=[VMEM] * 3,
+        in_specs=[VMEM] * 2,
         out_specs=VMEM,
-        input_output_aliases={2: 0},
+        input_output_aliases={1: 0},
         compiler_params=small,
         cost_estimate=pl.CostEstimate(flops=1000000, bytes_accessed=800000, transcendentals=0),
-    )(ya, yb, field)
+    )(ya, field)
     xa = swap(xa, 0, False)
     xb = swap(xb, 0, True)
     face = f32((96, 128))
@@ -553,15 +557,15 @@
     )(xa, xb, field)
     za = swap(za, 2, False)
     zb = swap(zb, 2, True)
-    inner = pl.pallas_call(
+    inner, displ_out = pl.pallas_call(
         inner_kernel,
-        out_shape=f32((4, 16, 640)),
-        in_specs=[VMEM],
-        out_specs=VMEM,
-        scratch_shapes=[pltpu.VMEM((4, 9, 16, 128), F32)],
+        out_shape=(f32((4, 16, 640)), f32(flat)),
+        in_specs=[VMEM] * 2,
+        out_specs=(VMEM, HBM),
+        scratch_shapes=[pltpu.VMEM((4, 9, 16, 128), F32), pltpu.SemaphoreType.DMA],
         compiler_params=small,
         cost_estimate=pl.CostEstimate(flops=1000000, bytes_accessed=800000, transcendentals=0),
-    )(field)
+    )(field, displ_new)
     veloc_out, accel_out = pl.pallas_call(
         end_kernel,
         out_shape=(f32(flat), f32(flat)),

time: 29.5 us -> 29.1 us (0.986)
  waiting for transfers between devices: 4.13 us -> 3.06 us
  starting transfers between devices: 16.1 us -> 17.1 us
  Pallas kernels: 8.57 us -> 8.05 us
    ppermute x1, starting transfers between devices: 1.3 us -> 3.63 us  [body(): passed = lax.ppermute(ya, 'gy', hops)]
    ppermute x5, waiting for transfers between devices: 3.99 us -> 2.23 us  [swap(): return lax.ppermute(value, axes, pairs)]
    ppermute x5, starting transfers between devices: 14.8 us -> 13.5 us  [swap(): return lax.ppermute(value, axes, pairs)]
    ppermute x1, waiting for transfers between devices: 0.14 us -> 0.83 us  [body(): passed = lax.ppermute(ya, 'gy', hops)]
    pallas_call x4, Pallas kernels: 3.51 us -> 3.19 us  [the longest x1 1.83 us: body(): pl.pallas_call(field_kernel, out_shape=f32((FROWS, 128)), in_specs=[VMEM]...]
  transfers between devices with their start and end apart: 6 -> 6, of which waited for: 4 -> 3; matrix products, arithmetic and copies ran while one was open for 0% -> 0% of each run, Pallas kernels for 11% -> 10%
where the time goes in v4:
time: 29.1 us; the launch traced here: 29 us
  starting transfers between devices  17.1 us (59%)
  Pallas kernels  8.05 us (28%)
  waiting for transfers between devices  3.06 us (11%)
  between operations  0.7 us (2%)
    ppermute x5, starting transfers between devices, swap(): return lax.ppermute(value, axes, pairs)  13.5 us
    pallas_call x1, Pallas kernels, body(): pl.pallas_call(force_kernel, out_shape=(f32((4, 200, 128)), jax.ShapeDtyp...  3.67 us
    ppermute x1, starting transfers between devices, body(): passed = lax.ppermute(ya, 'gy', hops)  3.63 us
    ppermute x5, waiting for transfers between devices, swap(): return lax.ppermute(value, axes, pairs)  2.23 us
    pallas_call x1, Pallas kernels, body(): pl.pallas_call(field_kernel, out_shape=f32((FROWS, 128)), in_specs=[VMEM]...  1.83 us
    pallas_call x1, Pallas kernels, body(): pl.pallas_call(end_kernel, out_shape=(f32(flat), f32(flat)), in_specs=[VM...  1.1 us
    ppermute x1, waiting for transfers between devices, body(): passed = lax.ppermute(ya, 'gy', hops)  0.83 us
    pallas_call x1, Pallas kernels, body(): pl.pallas_call(inner_kernel, out_shape=(f32((4, 16, 640)), f32(flat)), in...  0.66 us
  transfers between devices with their start and end apart: 6, of which 3 were waited for; matrix products, arithmetic and copies ran while one was open for 0% of the time, Pallas kernels for 10%

profile of v4, /device:TPU:1, one launch (start us, length us, event | category | flops | bytes accessed | tf_op | source)
XLA Modules:
  0.0 29.0 jit_solution(13757112330122074747)
XLA Ops:
  0.6 3.7 %shard_map.130 = (f32[4,200,128]{2,1,0:T(8,128)S(1)}, s32[8,128]{1,0:T(8,128)S(1)}, f32[24,128]{1,0:T(8,128)S(1)}, f32[3,1,9945]{2,1,0:T(1,128)S(1)}, f32[3,1,9945]{2,1,0:T(1,128)S(1)}) custom-call(f32[3,1,9945]{2,1,0:T(1,128)} %bitcast.19, f32[3,1,9945]{2,1,0:T(1,128)} %bitcast.20, f32[3,1,9945]{2,1,0:T(1,128)} %bitcast.21, s32[125,1,128]{2,1,0:T(1,128)} %bitcast.22, ...), custom_call_target="tpu_custom_call" | custom-call | tf_op jit(solution)/shard_map/pallas_call | solution.py:496
  4.3 3.6 %collective-permute-start = (f32[24,128]{1,0:T(8,128)S(1)}, f32[24,128]{1,0:T(8,128)S(1)}, u32[]{:S(2)}, u32[]{:S(2)}) collective-permute-start(f32[24,128]{1,0:T(8,128)S(1)} %get-tuple-element.17), channel_id=1, source_target_pairs={{0,48},{8,24},{16,0},{24,40},{32,16},{40,56},{48,32},{56,8},{1,49}... | collective-permute-start | bytes 36872 | tf_op jit(solution)/shard_map/ppermute | solution.py:520
  7.9 0.8 %collective-permute-done = f32[24,128]{1,0:T(8,128)S(1)} collective-permute-done((f32[24,128]{1,0:T(8,128)S(1)}, f32[24,128]{1,0:T(8,128)S(1)}, u32[]{:S(2)}, u32[]{:S(2)}) %collective-permute-start) | collective-permute-done | bytes 12320 | tf_op jit(solution)/shard_map/ppermute | solution.py:520
  8.8 7.2 %collective-permute-start.1 = (f32[24,128]{1,0:T(8,128)S(1)}, f32[24,128]{1,0:T(8,128)S(1)}, u32[]{:S(2)}, u32[]{:S(2)}) collective-permute-start(f32[24,128]{1,0:T(8,128)S(1)} %broadcast_select_fusion), channel_id=1, source_target_pairs={{0,8},{1,9},{2,10},{3,11},{4,12},{5,13},{6,14},{7,15},{8,0},{9,1},... | collective-permute-start | bytes 36872 | tf_op jit(solution)/shard_map/ppermute | solution.py:476
  15.9 1.8 %shard_map.131.f_ref.f_in = f32[960,128]{1,0:T(8,128)S(1)} custom-call(f32[4,200,128]{2,1,0:T(8,128)S(1)} %get-tuple-element.18.t_ref, s32[8,128]{1,0:T(8,128)S(1)} %get-tuple-element.19.o_ref), custom_call_target="tpu_custom_call" | custom-call | flops 4000000 | bytes 800000 | tf_op jit(solution)/shard_map/pallas_call | solution.py:522
  17.8 0.0 collective-permute-done.1.y_ref
  17.8 0.2 shard_map.132
  18.0 0.8 %collective-permute-start.2 = (f32[40,128]{1,0:T(8,128)S(1)}, f32[40,128]{1,0:T(8,128)S(1)}, u32[]{:S(2)}, u32[]{:S(2)}) collective-permute-start(f32[40,128]{1,0:T(8,128)S(1)} %get-tuple-element.20), channel_id=1, source_target_pairs={{0,64},{1,65},{2,66},{3,67},{4,68},{5,69},{6,70},{7,71},{8,72},{9,... | collective-permute-start | bytes 61448 | tf_op jit(solution)/shard_map/ppermute | solution.py:476
  18.8 2.3 %collective-permute-start.3 = (f32[40,128]{1,0:T(8,128)S(1)}, f32[40,128]{1,0:T(8,128)S(1)}, u32[]{:S(2)}, u32[]{:S(2)}) collective-permute-start(f32[40,128]{1,0:T(8,128)S(1)} %get-tuple-element.21), channel_id=1, source_target_pairs={{0,1},{1,0},{2,3},{3,2},{4,5},{5,4},{6,7},{7,6},{8,9},{9,8},{10,11... | collective-permute-start | bytes 61448 | tf_op jit(solution)/shard_map/ppermute | solution.py:476
  21.1 0.5 %shard_map.133.f_in = f32[960,128]{1,0:T(8,128)S(1)} custom-call(f32[24,128]{1,0:T(8,128)S(1)} %collective-permute-done.1.y_ref, f32[960,128]{1,0:T(8,128)S(1)} %shard_map.131.f_ref.f_in), custom_call_target="tpu_custom_call", output_to_operand_aliasing={{}: (1, {})} | custom-call | flops 1000000 | bytes 800000 | tf_op jit(solution)/shard_map/pallas_call | solution.py:538
  21.7 0.0 collective-permute-done.2.xa_ref
  21.7 0.3 %collective-permute-done.3.xb_ref = f32[40,128]{1,0:T(8,128)S(1)} collective-permute-done((f32[40,128]{1,0:T(8,128)S(1)}, f32[40,128]{1,0:T(8,128)S(1)}, u32[]{:S(2)}, u32[]{:S(2)}) %collective-permute-start.3) | collective-permute-done | bytes 20512 | tf_op jit(solution)/shard_map/ppermute | solution.py:476
  22.0 0.1 shard_map.134
  22.1 2.0 %collective-permute-start.4 = (f32[96,128]{1,0:T(8,128)S(1)}, f32[96,128]{1,0:T(8,128)S(1)}, u32[]{:S(2)}, u32[]{:S(2)}) collective-permute-start(f32[96,128]{1,0:T(8,128)S(1)} %get-tuple-element.25), channel_id=1, source_target_pairs={{0,1},{1,0},{2,3},{3,2},{4,5},{5,4},{6,7},{7,6},{8,9},{9,8},{10,11... | collective-permute-start | bytes 147464 | tf_op jit(solution)/shard_map/ppermute | solution.py:476
  24.1 1.2 %collective-permute-start.5 = (f32[96,128]{1,0:T(8,128)S(1)}, f32[96,128]{1,0:T(8,128)S(1)}, u32[]{:S(2)}, u32[]{:S(2)}) collective-permute-start(f32[96,128]{1,0:T(8,128)S(1)} %get-tuple-element.26), channel_id=1, source_target_pairs={{0,64},{1,2},{2,1},{3,4},{4,3},{5,6},{6,5},{7,71},{8,72},{9,10},{1... | collective-permute-start | bytes 147464 | tf_op jit(solution)/shard_map/ppermute | solution.py:476
  25.3 0.7 %shard_map.135 = (f32[4,16,640]{2,1,0:T(8,128)S(1)}, f32[3,1,9945]{2,1,0:T(1,128)}) custom-call(f32[960,128]{1,0:T(8,128)S(1)} %get-tuple-element.22.f_ref, f32[3,1,9945]{2,1,0:T(1,128)S(1)} %get-tuple-element.23.d_ref), custom_call_target="tpu_custom_call" | custom-call | flops 1000000 | bytes 800000 | tf_op jit(solution)/shard_map/pallas_call | solution.py:560
  25.9 0.0 collective-permute-done.4.za_ref
  25.9 1.9 %collective-permute-done.5.zb_ref = f32[96,128]{1,0:T(8,128)S(1)} collective-permute-done((f32[96,128]{1,0:T(8,128)S(1)}, f32[96,128]{1,0:T(8,128)S(1)}, u32[]{:S(2)}, u32[]{:S(2)}) %collective-permute-start.5) | collective-permute-done | bytes 49184 | tf_op jit(solution)/shard_map/ppermute | solution.py:476
  27.9 1.1 %shard_map.136 = (f32[3,1,9945]{2,1,0:T(1,128)}, f32[3,1,9945]{2,1,0:T(1,128)}) custom-call(f32[96,128]{1,0:T(8,128)S(1)} %collective-permute-done.4.za_ref, f32[96,128]{1,0:T(8,128)S(1)} %collective-permute-done.5.zb_ref, f32[960,128]{1,0:T(8,128)S(1)} %get-tuple-element.22.f_ref, f32[3,1,9945]{2,1,0:T(1,128)S(1)} %get-tuple-element.27.vh_ref, ...), custom_call_target="tpu_custom_call" | custom-call | tf_op jit(solution)/shard_map/pallas_call | solution.py:569
  (2 shorter events, 0.0 us)
Async XLA Ops:
  4.3 4.5 %collective-permute-start = (f32[24,128]{1,0:T(8,128)S(1)}, f32[24,128]{1,0:T(8,128)S(1)}, u32[]{:S(2)}, u32[]{:S(2)}) collective-permute-start(f32[24,128]{1,0:T(8,128)S(1)} %get-tuple-element.17), channel_id=1, source_target_pairs={{0,48},{8,24},{16,0},{24,40},{32,16},{40,56},{48,32},{56,8},{1,49}... | collective-permute-start | bytes 36872 | tf_op jit(solution)/shard_map/ppermute | solution.py:520
  8.8 9.0 %collective-permute-start.1 = (f32[24,128]{1,0:T(8,128)S(1)}, f32[24,128]{1,0:T(8,128)S(1)}, u32[]{:S(2)}, u32[]{:S(2)}) collective-permute-start(f32[24,128]{1,0:T(8,128)S(1)} %broadcast_select_fusion), channel_id=1, source_target_pairs={{0,8},{1,9},{2,10},{3,11},{4,12},{5,13},{6,14},{7,15},{8,0},{9,1},... | collective-permute-start | bytes 36872 | tf_op jit(solution)/shard_map/ppermute | solution.py:476
  18.0 3.7 %collective-permute-start.2 = (f32[40,128]{1,0:T(8,128)S(1)}, f32[40,128]{1,0:T(8,128)S(1)}, u32[]{:S(2)}, u32[]{:S(2)}) collective-permute-start(f32[40,128]{1,0:T(8,128)S(1)} %get-tuple-element.20), channel_id=1, source_target_pairs={{0,64},{1,65},{2,66},{3,67},{4,68},{5,69},{6,70},{7,71},{8,72},{9,... | collective-permute-start | bytes 61448 | tf_op jit(solution)/shard_map/ppermute | solution.py:476
  18.8 3.2 %collective-permute-start.3 = (f32[40,128]{1,0:T(8,128)S(1)}, f32[40,128]{1,0:T(8,128)S(1)}, u32[]{:S(2)}, u32[]{:S(2)}) collective-permute-start(f32[40,128]{1,0:T(8,128)S(1)} %get-tuple-element.21), channel_id=1, source_target_pairs={{0,1},{1,0},{2,3},{3,2},{4,5},{5,4},{6,7},{7,6},{8,9},{9,8},{10,11... | collective-permute-start | bytes 61448 | tf_op jit(solution)/shard_map/ppermute | solution.py:476
  22.1 3.9 %collective-permute-start.4 = (f32[96,128]{1,0:T(8,128)S(1)}, f32[96,128]{1,0:T(8,128)S(1)}, u32[]{:S(2)}, u32[]{:S(2)}) collective-permute-start(f32[96,128]{1,0:T(8,128)S(1)} %get-tuple-element.25), channel_id=1, source_target_pairs={{0,1},{1,0},{2,3},{3,2},{4,5},{5,4},{6,7},{7,6},{8,9},{9,8},{10,11... | collective-permute-start | bytes 147464 | tf_op jit(solution)/shard_map/ppermute | solution.py:476
  24.1 3.8 %collective-permute-start.5 = (f32[96,128]{1,0:T(8,128)S(1)}, f32[96,128]{1,0:T(8,128)S(1)}, u32[]{:S(2)}, u32[]{:S(2)}) collective-permute-start(f32[96,128]{1,0:T(8,128)S(1)} %get-tuple-element.26), channel_id=1, source_target_pairs={{0,64},{1,2},{2,1},{3,4},{4,3},{5,6},{6,5},{7,71},{8,72},{9,10},{1... | collective-permute-start | bytes 147464 | tf_op jit(solution)/shard_map/ppermute | solution.py:476

commit v5 on v4

--- a/solution.py
+++ b/solution.py
@@ -518,7 +518,6 @@
     count = lax.axis_size("gy")
     hops = [(i, (i - 2) % count if i % 2 == 0 else (i + 2) % count) for i in range(count)]
     passed = lax.ppermute(ya, "gy", hops)
-    ya = swap(jnp.where(lanes((XPAD, 128)) < 64, ya, passed), 1, False)
     field = pl.pallas_call(
         field_kernel,
         out_shape=f32((FROWS, 128)),
@@ -527,6 +526,8 @@
         compiler_params=small,
         cost_estimate=pl.CostEstimate(flops=4000000, bytes_accessed=800000, transcendentals=0),
     )(terms, slots)
+    passed, field = lax.optimization_barrier((passed, field))
+    ya = swap(jnp.where(lanes((XPAD, 128)) < 64, ya, passed), 1, False)
     face = f32((40, 128))
     xa, xb = pl.pallas_call(
         x_kernel,

time: 29.1 us -> 28.9 us (level)
  starting transfers between devices: 17.1 us -> 16.7 us
    ppermute x5, waiting for transfers between devices: 2.23 us -> 3.32 us  [swap(): return lax.ppermute(value, axes, pairs)]
    ppermute x1, waiting for transfers between devices: 0.83 us -> 0.01 us  [body(): passed = lax.ppermute(ya, 'gy', hops)]
    ppermute x5, starting transfers between devices: 13.5 us -> 13.1 us  [swap(): return lax.ppermute(value, axes, pairs)]
where the time goes in v5:
time: 28.9 us; the launch traced here: 28.8 us
  starting transfers between devices  16.7 us (58%)
  Pallas kernels  8.05 us (28%)
  waiting for transfers between devices  3.33 us (12%)
  between operations  0.7 us (2%)
    ppermute x5, starting transfers between devices, swap(): return lax.ppermute(value, axes, pairs)  13.1 us
    pallas_call x1, Pallas kernels, body(): pl.pallas_call(force_kernel, out_shape=(f32((4, 200, 128)), jax.ShapeDtyp...  3.67 us
    ppermute x1, starting transfers between devices, body(): passed = lax.ppermute(ya, 'gy', hops)  3.63 us
    ppermute x5, waiting for transfers between devices, swap(): return lax.ppermute(value, axes, pairs)  3.32 us
    pallas_call x1, Pallas kernels, body(): pl.pallas_call(field_kernel, out_shape=f32((FROWS, 128)), in_specs=[VMEM]...  1.83 us
    pallas_call x1, Pallas kernels, body(): pl.pallas_call(end_kernel, out_shape=(f32(flat), f32(flat)), in_specs=[VM...  1.1 us
    pallas_call x1, Pallas kernels, body(): pl.pallas_call(inner_kernel, out_shape=(f32((4, 16, 640)), f32(flat)), in...  0.66 us
  transfers between devices with their start and end apart: 6, of which 3 were waited for; matrix products, arithmetic and copies ran while one was open for 0% of the time, Pallas kernels for 10%

profile of v5, /device:TPU:1, one launch (start us, length us, event | category | flops | bytes accessed | tf_op | source)
XLA Modules:
  0.0 28.8 jit_solution(9171803372696015813)
XLA Ops:
  0.6 3.7 %shard_map.130 = (f32[4,200,128]{2,1,0:T(8,128)S(1)}, s32[8,128]{1,0:T(8,128)S(1)}, f32[24,128]{1,0:T(8,128)S(1)}, f32[3,1,9945]{2,1,0:T(1,128)S(1)}, f32[3,1,9945]{2,1,0:T(1,128)S(1)}) custom-call(f32[3,1,9945]{2,1,0:T(1,128)} %bitcast.19, f32[3,1,9945]{2,1,0:T(1,128)} %bitcast.20, f32[3,1,9945]{2,1,0:T(1,128)} %bitcast.21, s32[125,1,128]{2,1,0:T(1,128)} %bitcast.22, ...), custom_call_target="tpu_custom_call" | custom-call | tf_op jit(solution)/shard_map/pallas_call | solution.py:496
  4.3 3.6 %collective-permute-start = (f32[24,128]{1,0:T(8,128)S(1)}, f32[24,128]{1,0:T(8,128)S(1)}, u32[]{:S(2)}, u32[]{:S(2)}) collective-permute-start(f32[24,128]{1,0:T(8,128)S(1)} %get-tuple-element.19), channel_id=1, source_target_pairs={{0,48},{8,24},{16,0},{24,40},{32,16},{40,56},{48,32},{56,8},{1,49}... | collective-permute-start | bytes 36872 | tf_op jit(solution)/shard_map/ppermute | solution.py:520
  7.9 1.8 %shard_map.131.f_ref.f_in = f32[960,128]{1,0:T(8,128)S(1)} custom-call(f32[4,200,128]{2,1,0:T(8,128)S(1)} %get-tuple-element.20.t_ref, s32[8,128]{1,0:T(8,128)S(1)} %get-tuple-element.21.o_ref), custom_call_target="tpu_custom_call" | custom-call | flops 4000000 | bytes 800000 | tf_op jit(solution)/shard_map/pallas_call | solution.py:521
  9.8 0.0 collective-permute-done
  9.8 6.1 %collective-permute-start.1 = (f32[24,128]{1,0:T(8,128)S(1)}, f32[24,128]{1,0:T(8,128)S(1)}, u32[]{:S(2)}, u32[]{:S(2)}) collective-permute-start(f32[24,128]{1,0:T(8,128)S(1)} %broadcast_select_fusion), channel_id=1, source_target_pairs={{0,8},{1,9},{2,10},{3,11},{4,12},{5,13},{6,14},{7,15},{8,0},{9,1},... | collective-permute-start | bytes 36872 | tf_op jit(solution)/shard_map/ppermute | solution.py:476
  15.9 1.1 %collective-permute-done.1.y_ref = f32[24,128]{1,0:T(8,128)S(1)} collective-permute-done((f32[24,128]{1,0:T(8,128)S(1)}, f32[24,128]{1,0:T(8,128)S(1)}, u32[]{:S(2)}, u32[]{:S(2)}) %collective-permute-start.1) | collective-permute-done | bytes 12320 | tf_op jit(solution)/shard_map/ppermute | solution.py:476
  17.0 0.2 shard_map.132
  17.2 1.0 %collective-permute-start.2 = (f32[40,128]{1,0:T(8,128)S(1)}, f32[40,128]{1,0:T(8,128)S(1)}, u32[]{:S(2)}, u32[]{:S(2)}) collective-permute-start(f32[40,128]{1,0:T(8,128)S(1)} %get-tuple-element.24), channel_id=1, source_target_pairs={{0,64},{1,65},{2,66},{3,67},{4,68},{5,69},{6,70},{7,71},{8,72},{9,... | collective-permute-start | bytes 61448 | tf_op jit(solution)/shard_map/ppermute | solution.py:476
  18.2 2.7 %collective-permute-start.3 = (f32[40,128]{1,0:T(8,128)S(1)}, f32[40,128]{1,0:T(8,128)S(1)}, u32[]{:S(2)}, u32[]{:S(2)}) collective-permute-start(f32[40,128]{1,0:T(8,128)S(1)} %get-tuple-element.25), channel_id=1, source_target_pairs={{0,1},{1,0},{2,3},{3,2},{4,5},{5,4},{6,7},{7,6},{8,9},{9,8},{10,11... | collective-permute-start | bytes 61448 | tf_op jit(solution)/shard_map/ppermute | solution.py:476
  20.9 0.5 %shard_map.133.f_in = f32[960,128]{1,0:T(8,128)S(1)} custom-call(f32[24,128]{1,0:T(8,128)S(1)} %collective-permute-done.1.y_ref, f32[960,128]{1,0:T(8,128)S(1)} %shard_map.131.f_ref.f_in), custom_call_target="tpu_custom_call", output_to_operand_aliasing={{}: (1, {})} | custom-call | flops 1000000 | bytes 800000 | tf_op jit(solution)/shard_map/pallas_call | solution.py:539
  21.5 0.0 collective-permute-done.2.xa_ref
  21.5 0.3 %collective-permute-done.3.xb_ref = f32[40,128]{1,0:T(8,128)S(1)} collective-permute-done((f32[40,128]{1,0:T(8,128)S(1)}, f32[40,128]{1,0:T(8,128)S(1)}, u32[]{:S(2)}, u32[]{:S(2)}) %collective-permute-start.3) | collective-permute-done | bytes 20512 | tf_op jit(solution)/shard_map/ppermute | solution.py:476
  21.8 0.1 shard_map.134
  21.9 2.0 %collective-permute-start.4 = (f32[96,128]{1,0:T(8,128)S(1)}, f32[96,128]{1,0:T(8,128)S(1)}, u32[]{:S(2)}, u32[]{:S(2)}) collective-permute-start(f32[96,128]{1,0:T(8,128)S(1)} %get-tuple-element.29), channel_id=1, source_target_pairs={{0,1},{1,0},{2,3},{3,2},{4,5},{5,4},{6,7},{7,6},{8,9},{9,8},{10,11... | collective-permute-start | bytes 147464 | tf_op jit(solution)/shard_map/ppermute | solution.py:476
  23.9 1.2 %collective-permute-start.5 = (f32[96,128]{1,0:T(8,128)S(1)}, f32[96,128]{1,0:T(8,128)S(1)}, u32[]{:S(2)}, u32[]{:S(2)}) collective-permute-start(f32[96,128]{1,0:T(8,128)S(1)} %get-tuple-element.30), channel_id=1, source_target_pairs={{0,64},{1,2},{2,1},{3,4},{4,3},{5,6},{6,5},{7,71},{8,72},{9,10},{1... | collective-permute-start | bytes 147464 | tf_op jit(solution)/shard_map/ppermute | solution.py:476
  25.1 0.7 %shard_map.135 = (f32[4,16,640]{2,1,0:T(8,128)S(1)}, f32[3,1,9945]{2,1,0:T(1,128)}) custom-call(f32[960,128]{1,0:T(8,128)S(1)} %get-tuple-element.26.f_ref, f32[3,1,9945]{2,1,0:T(1,128)S(1)} %get-tuple-element.27.d_ref), custom_call_target="tpu_custom_call" | custom-call | flops 1000000 | bytes 800000 | tf_op jit(solution)/shard_map/pallas_call | solution.py:561
  25.8 0.0 collective-permute-done.4.za_ref
  25.8 1.9 %collective-permute-done.5.zb_ref = f32[96,128]{1,0:T(8,128)S(1)} collective-permute-done((f32[96,128]{1,0:T(8,128)S(1)}, f32[96,128]{1,0:T(8,128)S(1)}, u32[]{:S(2)}, u32[]{:S(2)}) %collective-permute-start.5) | collective-permute-done | bytes 49184 | tf_op jit(solution)/shard_map/ppermute | solution.py:476
  27.7 1.1 %shard_map.136 = (f32[3,1,9945]{2,1,0:T(1,128)}, f32[3,1,9945]{2,1,0:T(1,128)}) custom-call(f32[96,128]{1,0:T(8,128)S(1)} %collective-permute-done.4.za_ref, f32[96,128]{1,0:T(8,128)S(1)} %collective-permute-done.5.zb_ref, f32[960,128]{1,0:T(8,128)S(1)} %get-tuple-element.26.f_ref, f32[3,1,9945]{2,1,0:T(1,128)S(1)} %get-tuple-element.31.vh_ref, ...), custom_call_target="tpu_custom_call" | custom-call | tf_op jit(solution)/shard_map/pallas_call | solution.py:570
  (2 shorter events, 0.0 us)
Async XLA Ops:
  4.3 5.5 %collective-permute-start = (f32[24,128]{1,0:T(8,128)S(1)}, f32[24,128]{1,0:T(8,128)S(1)}, u32[]{:S(2)}, u32[]{:S(2)}) collective-permute-start(f32[24,128]{1,0:T(8,128)S(1)} %get-tuple-element.19), channel_id=1, source_target_pairs={{0,48},{8,24},{16,0},{24,40},{32,16},{40,56},{48,32},{56,8},{1,49}... | collective-permute-start | bytes 36872 | tf_op jit(solution)/shard_map/ppermute | solution.py:520
  9.8 7.2 %collective-permute-start.1 = (f32[24,128]{1,0:T(8,128)S(1)}, f32[24,128]{1,0:T(8,128)S(1)}, u32[]{:S(2)}, u32[]{:S(2)}) collective-permute-start(f32[24,128]{1,0:T(8,128)S(1)} %broadcast_select_fusion), channel_id=1, source_target_pairs={{0,8},{1,9},{2,10},{3,11},{4,12},{5,13},{6,14},{7,15},{8,0},{9,1},... | collective-permute-start | bytes 36872 | tf_op jit(solution)/shard_map/ppermute | solution.py:476
  17.2 4.3 %collective-permute-start.2 = (f32[40,128]{1,0:T(8,128)S(1)}, f32[40,128]{1,0:T(8,128)S(1)}, u32[]{:S(2)}, u32[]{:S(2)}) collective-permute-start(f32[40,128]{1,0:T(8,128)S(1)} %get-tuple-element.24), channel_id=1, source_target_pairs={{0,64},{1,65},{2,66},{3,67},{4,68},{5,69},{6,70},{7,71},{8,72},{9,... | collective-permute-start | bytes 61448 | tf_op jit(solution)/shard_map/ppermute | solution.py:476
  18.2 3.5 %collective-permute-start.3 = (f32[40,128]{1,0:T(8,128)S(1)}, f32[40,128]{1,0:T(8,128)S(1)}, u32[]{:S(2)}, u32[]{:S(2)}) collective-permute-start(f32[40,128]{1,0:T(8,128)S(1)} %get-tuple-element.25), channel_id=1, source_target_pairs={{0,1},{1,0},{2,3},{3,2},{4,5},{5,4},{6,7},{7,6},{8,9},{9,8},{10,11... | collective-permute-start | bytes 61448 | tf_op jit(solution)/shard_map/ppermute | solution.py:476
  21.9 3.9 %collective-permute-start.4 = (f32[96,128]{1,0:T(8,128)S(1)}, f32[96,128]{1,0:T(8,128)S(1)}, u32[]{:S(2)}, u32[]{:S(2)}) collective-permute-start(f32[96,128]{1,0:T(8,128)S(1)} %get-tuple-element.29), channel_id=1, source_target_pairs={{0,1},{1,0},{2,3},{3,2},{4,5},{5,4},{6,7},{7,6},{8,9},{9,8},{10,11... | collective-permute-start | bytes 147464 | tf_op jit(solution)/shard_map/ppermute | solution.py:476
  23.9 3.8 %collective-permute-start.5 = (f32[96,128]{1,0:T(8,128)S(1)}, f32[96,128]{1,0:T(8,128)S(1)}, u32[]{:S(2)}, u32[]{:S(2)}) collective-permute-start(f32[96,128]{1,0:T(8,128)S(1)} %get-tuple-element.30), channel_id=1, source_target_pairs={{0,64},{1,2},{2,1},{3,4},{4,3},{5,6},{6,5},{7,71},{8,72},{9,10},{1... | collective-permute-start | bytes 147464 | tf_op jit(solution)/shard_map/ppermute | solution.py:476

commit v6 on v5

--- a/solution.py
+++ b/solution.py
@@ -88,8 +88,8 @@
 
 def force_kernel(
     d_hbm, v_hbm, a_hbm, n_hbm, m_hbm, j_hbm, l_hbm, s_hbm, r_hbm, fw_hbm, bw_hbm,
-    t_ref, o_ref, y_ref, vh_ref, pos_s,
-    d_s, v_s, a_s, n_s, m_s, j_s, l_s, s_s, r_s, fw_s, bw_s,
+    t_ref, o_ref, y_ref, v_s, a_s, pos_s,
+    d_s, n_s, m_s, j_s, l_s, s_s, r_s, fw_s, bw_s,
     grid_s, nodal_s, local_s, grad_s, fluxh_s, fluxl_s, sems,
 ):
     copies = []
@@ -106,13 +106,12 @@
         copy = pltpu.make_async_copy(src, dst, sems.at[at])
         copy.start()
         copies.append(copy)
-    for at in range(10):
-        copies[at].wait()
-    accel = a_s[...]
-    veloc = v_s[...]
-    pos_s[...] = d_s[...] + time_step * veloc + HALF_SQ * accel
-    vh_ref[...] = veloc + HALF * accel
     lane = lanes()
+    for m in range(4):
+        t_ref[m, 128:200, :] = jnp.zeros((72, 128), F32)
+    for m in range(3):
+        local_s[m, 120:128, :] = jnp.zeros((8, 128), F32)
+    copies[0].wait()
 
     corner = jnp.broadcast_to(n_s[0], (8, 128))
     elem_x = (
@@ -130,6 +129,10 @@
     slot_index = lax.broadcasted_iota(jnp.int32, (128, 128), 0).astype(F32)
     slot_of = jnp.sum(jnp.where(hit, slot_index, 0.0), axis=0, keepdims=True)
     slot_of = jnp.broadcast_to(slot_of, (8, 128)).astype(jnp.int32)
+
+    for at in range(1, 10):
+        copies[at].wait()
+    pos_s[...] = d_s[...] + time_step * v_s[...] + HALF_SQ * a_s[...]
 
     for m in range(3):
         for x in range(NX):
@@ -162,7 +165,6 @@
     inner = 64 * elem_z + 4 * elem_y
     outer = 16 * elem_z + elem_y
     for m in range(3):
-        local_s[m, 120:128, :] = jnp.zeros((8, 128), F32)
         for c in range(5):
             near = [nodal_s[m, c, 4 * x : 4 * x + 8, :] for x in range(4)]
             last = [nodal_s[m, 5 + c // 4, 4 * x : 4 * x + 8, :] for x in range(4)]
@@ -221,8 +223,6 @@
     terms = both[:128] + both[128:] + dot(bw_s[0:128, :], fluxl_s[...])
     for m in range(3):
         t_ref[m, 0:128, :] = terms[:, 128 * m : 128 * m + 128]
-    for m in range(4):
-        t_ref[m, 128:200, :] = jnp.zeros((72, 128), F32)
     o_ref[...] = slot_of
 
     edge = take(slot_of, 16 * (lane & 7) + 15 * ((lane >> 3) & 1))
@@ -381,9 +381,10 @@
     return spots
 
 
-def inner_kernel(f_ref, d_ref, grid_ref, d_out, acc_s, sem):
+def inner_kernel(f_ref, d_ref, v_ref, a_ref, grid_ref, vh_ref, d_out, acc_s, sem):
     out_copy = pltpu.make_async_copy(d_ref, d_out, sem)
     out_copy.start()
+    vh_ref[...] = v_ref[...] + HALF * a_ref[...]
     for z in range(1, 8):
         for tile in range(3):
             rows = [(m * 9 + z) * XPAD + 8 * tile for m in range(4)]
@@ -482,8 +483,7 @@
     points = (125, 1, 128)
     tables = [jnp.asarray(table) for table in operator_tables()]
     scratch = [
-        pltpu.VMEM(flat, F32), pltpu.VMEM(flat, F32), pltpu.VMEM(flat, F32),
-        pltpu.VMEM((1, 1, 128), jnp.int32),
+        pltpu.VMEM(flat, F32), pltpu.VMEM((1, 1, 128), jnp.int32),
         pltpu.VMEM((9, 128, 128), F32),
         pltpu.VMEM((128, 128), F32), pltpu.VMEM((128, 128), F32),
         pltpu.VMEM((128, 128), F32), pltpu.VMEM((128, 128), F32),
@@ -493,14 +493,14 @@
         pltpu.VMEM((384, 384), BF16), pltpu.VMEM((384, 384), BF16),
         pltpu.SemaphoreType.DMA((25,)),
     ]
-    terms, slots, ya, v_half, displ_new = pl.pallas_call(
+    terms, slots, ya, v_old, a_old, displ_new = pl.pallas_call(
         force_kernel,
         out_shape=(
             f32((4, 200, 128)), jax.ShapeDtypeStruct((8, 128), jnp.int32), f32((XPAD, 128)),
-            f32(flat), f32(flat),
+            f32(flat), f32(flat), f32(flat),
         ),
         in_specs=[HBM] * 11,
-        out_specs=(VMEM,) * 5,
+        out_specs=(VMEM,) * 6,
         scratch_shapes=scratch,
         compiler_params=pltpu.CompilerParams(vmem_limit_bytes=16 << 20),
     )(
@@ -558,15 +558,15 @@
     )(xa, xb, field)
     za = swap(za, 2, False)
     zb = swap(zb, 2, True)
-    inner, displ_out = pl.pallas_call(
+    inner, v_half, displ_out = pl.pallas_call(
         inner_kernel,
-        out_shape=(f32((4, 16, 640)), f32(flat)),
-        in_specs=[VMEM] * 2,
-        out_specs=(VMEM, HBM),
+        out_shape=(f32((4, 16, 640)), f32(flat), f32(flat)),
+        in_specs=[VMEM] * 4,
+        out_specs=(VMEM, VMEM, HBM),
         scratch_shapes=[pltpu.VMEM((4, 9, 16, 128), F32), pltpu.SemaphoreType.DMA],
         compiler_params=small,
         cost_estimate=pl.CostEstimate(flops=1000000, bytes_accessed=800000, transcendentals=0),
-    )(field, displ_new)
+    )(field, displ_new, v_old, a_old)
     veloc_out, accel_out = pl.pallas_call(
         end_kernel,
         out_shape=(f32(flat), f32(flat)),

time: 28.9 us -> 28.9 us (level)
  transfers between devices with their start and end apart: 6 -> 6, of which waited for: 3 -> 3; matrix products, arithmetic and copies ran while one was open for 0% -> 0% of each run, Pallas kernels for 10% -> 11%
where the time goes in v6:
time: 28.9 us; the launch traced here: 28.8 us
  starting transfers between devices  16.7 us (58%)
  Pallas kernels  8.06 us (28%)
  waiting for transfers between devices  3.31 us (11%)
  between operations  0.7 us (2%)
    ppermute x5, starting transfers between devices, swap(): return lax.ppermute(value, axes, pairs)  13.1 us
    pallas_call x1, Pallas kernels, body(): pl.pallas_call(force_kernel, out_shape=(f32((4, 200, 128)), jax.ShapeDtyp...  3.66 us
    ppermute x1, starting transfers between devices, body(): passed = lax.ppermute(ya, 'gy', hops)  3.63 us
    ppermute x5, waiting for transfers between devices, swap(): return lax.ppermute(value, axes, pairs)  3.31 us
    pallas_call x1, Pallas kernels, body(): pl.pallas_call(field_kernel, out_shape=f32((FROWS, 128)), in_specs=[VMEM]...  1.83 us
    pallas_call x1, Pallas kernels, body(): pl.pallas_call(end_kernel, out_shape=(f32(flat), f32(flat)), in_specs=[VM...  1.1 us
    pallas_call x1, Pallas kernels, body(): pl.pallas_call(inner_kernel, out_shape=(f32((4, 16, 640)), f32(flat), f32...  0.67 us
  transfers between devices with their start and end apart: 6, of which 3 were waited for; matrix products, arithmetic and copies ran while one was open for 0% of the time, Pallas kernels for 11%

profile of v6, /device:TPU:1, one launch (start us, length us, event | category | flops | bytes accessed | tf_op | source)
XLA Modules:
  0.0 28.8 jit_solution(1175683980099226428)
XLA Ops:
  0.6 3.7 %shard_map.130 = (f32[4,200,128]{2,1,0:T(8,128)S(1)}, s32[8,128]{1,0:T(8,128)S(1)}, f32[24,128]{1,0:T(8,128)S(1)}, f32[3,1,9945]{2,1,0:T(1,128)S(1)}, f32[3,1,99...) custom-call(f32[3,1,9945]{2,1,0:T(1,128)} %bitcast.19, f32[3,1,9945]{2,1,0:T(1,128)} %bitcast.20, f32[3,1,9945]{2,1,0:T(1,128)} %bitcast.21, ...), custom_call_target="tpu_custom_call" | custom-call | tf_op jit(solution)/shard_map/pallas_call | solution.py:496
  4.3 3.6 %collective-permute-start = (f32[24,128]{1,0:T(8,128)S(1)}, f32[24,128]{1,0:T(8,128)S(1)}, u32[]{:S(2)}, u32[]{:S(2)}) collective-permute-start(f32[24,128]{1,0:T(8,128)S(1)} %get-tuple-element.21), channel_id=1, source_target_pairs={{0,48},{8,24},{16,0},{24,40},{32,16},{40,56},{48,32},{56,8},{1,49}... | collective-permute-start | bytes 36872 | tf_op jit(solution)/shard_map/ppermute | solution.py:520
  7.9 1.8 %shard_map.131.f_ref.f_in = f32[960,128]{1,0:T(8,128)S(1)} custom-call(f32[4,200,128]{2,1,0:T(8,128)S(1)} %get-tuple-element.22.t_ref, s32[8,128]{1,0:T(8,128)S(1)} %get-tuple-element.23.o_ref), custom_call_target="tpu_custom_call" | custom-call | flops 4000000 | bytes 800000 | tf_op jit(solution)/shard_map/pallas_call | solution.py:521
  9.8 0.0 collective-permute-done
  9.8 6.1 %collective-permute-start.1 = (f32[24,128]{1,0:T(8,128)S(1)}, f32[24,128]{1,0:T(8,128)S(1)}, u32[]{:S(2)}, u32[]{:S(2)}) collective-permute-start(f32[24,128]{1,0:T(8,128)S(1)} %broadcast_select_fusion), channel_id=1, source_target_pairs={{0,8},{1,9},{2,10},{3,11},{4,12},{5,13},{6,14},{7,15},{8,0},{9,1},... | collective-permute-start | bytes 36872 | tf_op jit(solution)/shard_map/ppermute | solution.py:477
  15.9 1.1 %collective-permute-done.1.y_ref = f32[24,128]{1,0:T(8,128)S(1)} collective-permute-done((f32[24,128]{1,0:T(8,128)S(1)}, f32[24,128]{1,0:T(8,128)S(1)}, u32[]{:S(2)}, u32[]{:S(2)}) %collective-permute-start.1) | collective-permute-done | bytes 12320 | tf_op jit(solution)/shard_map/ppermute | solution.py:477
  17.0 0.2 shard_map.132
  17.2 1.0 %collective-permute-start.2 = (f32[40,128]{1,0:T(8,128)S(1)}, f32[40,128]{1,0:T(8,128)S(1)}, u32[]{:S(2)}, u32[]{:S(2)}) collective-permute-start(f32[40,128]{1,0:T(8,128)S(1)} %get-tuple-element.26), channel_id=1, source_target_pairs={{0,64},{1,65},{2,66},{3,67},{4,68},{5,69},{6,70},{7,71},{8,72},{9,... | collective-permute-start | bytes 61448 | tf_op jit(solution)/shard_map/ppermute | solution.py:477
  18.2 2.7 %collective-permute-start.3 = (f32[40,128]{1,0:T(8,128)S(1)}, f32[40,128]{1,0:T(8,128)S(1)}, u32[]{:S(2)}, u32[]{:S(2)}) collective-permute-start(f32[40,128]{1,0:T(8,128)S(1)} %get-tuple-element.27), channel_id=1, source_target_pairs={{0,1},{1,0},{2,3},{3,2},{4,5},{5,4},{6,7},{7,6},{8,9},{9,8},{10,11... | collective-permute-start | bytes 61448 | tf_op jit(solution)/shard_map/ppermute | solution.py:477
  20.9 0.5 %shard_map.133.f_in = f32[960,128]{1,0:T(8,128)S(1)} custom-call(f32[24,128]{1,0:T(8,128)S(1)} %collective-permute-done.1.y_ref, f32[960,128]{1,0:T(8,128)S(1)} %shard_map.131.f_ref.f_in), custom_call_target="tpu_custom_call", output_to_operand_aliasing={{}: (1, {})} | custom-call | flops 1000000 | bytes 800000 | tf_op jit(solution)/shard_map/pallas_call | solution.py:539
  21.5 0.0 collective-permute-done.2.xa_ref
  21.5 0.3 %collective-permute-done.3.xb_ref = f32[40,128]{1,0:T(8,128)S(1)} collective-permute-done((f32[40,128]{1,0:T(8,128)S(1)}, f32[40,128]{1,0:T(8,128)S(1)}, u32[]{:S(2)}, u32[]{:S(2)}) %collective-permute-start.3) | collective-permute-done | bytes 20512 | tf_op jit(solution)/shard_map/ppermute | solution.py:477
  21.8 0.1 shard_map.134
  21.9 2.0 %collective-permute-start.4 = (f32[96,128]{1,0:T(8,128)S(1)}, f32[96,128]{1,0:T(8,128)S(1)}, u32[]{:S(2)}, u32[]{:S(2)}) collective-permute-start(f32[96,128]{1,0:T(8,128)S(1)} %get-tuple-element.33), channel_id=1, source_target_pairs={{0,1},{1,0},{2,3},{3,2},{4,5},{5,4},{6,7},{7,6},{8,9},{9,8},{10,11... | collective-permute-start | bytes 147464 | tf_op jit(solution)/shard_map/ppermute | solution.py:477
  23.9 1.2 %collective-permute-start.5 = (f32[96,128]{1,0:T(8,128)S(1)}, f32[96,128]{1,0:T(8,128)S(1)}, u32[]{:S(2)}, u32[]{:S(2)}) collective-permute-start(f32[96,128]{1,0:T(8,128)S(1)} %get-tuple-element.34), channel_id=1, source_target_pairs={{0,64},{1,2},{2,1},{3,4},{4,3},{5,6},{6,5},{7,71},{8,72},{9,10},{1... | collective-permute-start | bytes 147464 | tf_op jit(solution)/shard_map/ppermute | solution.py:477
  25.1 0.7 %shard_map.135 = (f32[4,16,640]{2,1,0:T(8,128)S(1)}, f32[3,1,9945]{2,1,0:T(1,128)S(1)}, f32[3,1,9945]{2,1,0:T(1,128)}) custom-call(f32[960,128]{1,0:T(8,128)S(1)} %get-tuple-element.28.f_ref, f32[3,1,9945]{2,1,0:T(1,128)S(1)} %get-tuple-element.29.d_ref, f32[3,1,9945]{2,1,0:T(1,128)S(1)} %get-tuple-element.30.v_ref, f32[3,1,9945]{2,1,0:T(1,128)S(1)} %get-tuple-element.31.a_ref), custom_call_target="tpu_custom_call" | custom-call | flops 1000000 | bytes 800000 | tf_op jit(solution)/shard_map/pallas_call | solution.py:561
  25.8 0.0 collective-permute-done.4.za_ref
  25.8 1.9 %collective-permute-done.5.zb_ref = f32[96,128]{1,0:T(8,128)S(1)} collective-permute-done((f32[96,128]{1,0:T(8,128)S(1)}, f32[96,128]{1,0:T(8,128)S(1)}, u32[]{:S(2)}, u32[]{:S(2)}) %collective-permute-start.5) | collective-permute-done | bytes 49184 | tf_op jit(solution)/shard_map/ppermute | solution.py:477
  27.7 1.1 %shard_map.136 = (f32[3,1,9945]{2,1,0:T(1,128)}, f32[3,1,9945]{2,1,0:T(1,128)}) custom-call(f32[96,128]{1,0:T(8,128)S(1)} %collective-permute-done.4.za_ref, f32[96,128]{1,0:T(8,128)S(1)} %collective-permute-done.5.zb_ref, f32[960,128]{1,0:T(8,128)S(1)} %get-tuple-element.28.f_ref, f32[3,1,9945]{2,1,0:T(1,128)S(1)} %get-tuple-element.35.vh_ref, ...), custom_call_target="tpu_custom_call" | custom-call | tf_op jit(solution)/shard_map/pallas_call | solution.py:570
  (2 shorter events, 0.0 us)
Async XLA Ops:
  4.3 5.5 %collective-permute-start = (f32[24,128]{1,0:T(8,128)S(1)}, f32[24,128]{1,0:T(8,128)S(1)}, u32[]{:S(2)}, u32[]{:S(2)}) collective-permute-start(f32[24,128]{1,0:T(8,128)S(1)} %get-tuple-element.21), channel_id=1, source_target_pairs={{0,48},{8,24},{16,0},{24,40},{32,16},{40,56},{48,32},{56,8},{1,49}... | collective-permute-start | bytes 36872 | tf_op jit(solution)/shard_map/ppermute | solution.py:520
  9.8 7.2 %collective-permute-start.1 = (f32[24,128]{1,0:T(8,128)S(1)}, f32[24,128]{1,0:T(8,128)S(1)}, u32[]{:S(2)}, u32[]{:S(2)}) collective-permute-start(f32[24,128]{1,0:T(8,128)S(1)} %broadcast_select_fusion), channel_id=1, source_target_pairs={{0,8},{1,9},{2,10},{3,11},{4,12},{5,13},{6,14},{7,15},{8,0},{9,1},... | collective-permute-start | bytes 36872 | tf_op jit(solution)/shard_map/ppermute | solution.py:477
  17.2 4.3 %collective-permute-start.2 = (f32[40,128]{1,0:T(8,128)S(1)}, f32[40,128]{1,0:T(8,128)S(1)}, u32[]{:S(2)}, u32[]{:S(2)}) collective-permute-start(f32[40,128]{1,0:T(8,128)S(1)} %get-tuple-element.26), channel_id=1, source_target_pairs={{0,64},{1,65},{2,66},{3,67},{4,68},{5,69},{6,70},{7,71},{8,72},{9,... | collective-permute-start | bytes 61448 | tf_op jit(solution)/shard_map/ppermute | solution.py:477
  18.2 3.5 %collective-permute-start.3 = (f32[40,128]{1,0:T(8,128)S(1)}, f32[40,128]{1,0:T(8,128)S(1)}, u32[]{:S(2)}, u32[]{:S(2)}) collective-permute-start(f32[40,128]{1,0:T(8,128)S(1)} %get-tuple-element.27), channel_id=1, source_target_pairs={{0,1},{1,0},{2,3},{3,2},{4,5},{5,4},{6,7},{7,6},{8,9},{9,8},{10,11... | collective-permute-start | bytes 61448 | tf_op jit(solution)/shard_map/ppermute | solution.py:477
  21.9 3.9 %collective-permute-start.4 = (f32[96,128]{1,0:T(8,128)S(1)}, f32[96,128]{1,0:T(8,128)S(1)}, u32[]{:S(2)}, u32[]{:S(2)}) collective-permute-start(f32[96,128]{1,0:T(8,128)S(1)} %get-tuple-element.33), channel_id=1, source_target_pairs={{0,1},{1,0},{2,3},{3,2},{4,5},{5,4},{6,7},{7,6},{8,9},{9,8},{10,11... | collective-permute-start | bytes 147464 | tf_op jit(solution)/shard_map/ppermute | solution.py:477
  23.9 3.8 %collective-permute-start.5 = (f32[96,128]{1,0:T(8,128)S(1)}, f32[96,128]{1,0:T(8,128)S(1)}, u32[]{:S(2)}, u32[]{:S(2)}) collective-permute-start(f32[96,128]{1,0:T(8,128)S(1)} %get-tuple-element.34), channel_id=1, source_target_pairs={{0,64},{1,2},{2,1},{3,4},{4,3},{5,6},{6,5},{7,71},{8,72},{9,10},{1... | collective-permute-start | bytes 147464 | tf_op jit(solution)/shard_map/ppermute | solution.py:477

commit v7 on v6

--- a/solution.py
+++ b/solution.py
@@ -90,7 +90,7 @@
     d_hbm, v_hbm, a_hbm, n_hbm, m_hbm, j_hbm, l_hbm, s_hbm, r_hbm, fw_hbm, bw_hbm,
     t_ref, o_ref, y_ref, v_s, a_s, pos_s,
     d_s, n_s, m_s, j_s, l_s, s_s, r_s, fw_s, bw_s,
-    grid_s, nodal_s, local_s, grad_s, fluxh_s, fluxl_s, sems,
+    grid_s, nodal_s, local_s, grad_s, wide_s, fluxh_s, fluxl_s, sems,
 ):
     copies = []
     moves = [(n_hbm.at[pl.ds(0, 1)], n_s)]
@@ -132,11 +132,13 @@
 
     for at in range(1, 10):
         copies[at].wait()
-    pos_s[...] = d_s[...] + time_step * v_s[...] + HALF_SQ * a_s[...]
+    moved = d_s[...] + time_step * v_s[...] + HALF_SQ * a_s[...]
+    pos_s[...] = moved
+    wide_s[0:3] = moved
 
     for m in range(3):
         for x in range(NX):
-            value = pos_s[m, :, pl.ds(ROW * x, ROW)]
+            value = wide_s[m, :, pl.ds(ROW * x, ROW)]
             if x < 16:
                 grid_s[m, x : x + 1, :ROW] = value
             else:
@@ -176,7 +178,7 @@
                 local_s[m, pl.ds(5 * b + c, 5, stride=25), :] = got[:5]
 
     copies[10].wait()
-    local = jnp.concatenate([local_s[m] for m in range(3)], axis=1)
+    local = jnp.concatenate([local_s[m, 0:128, :] for m in range(3)], axis=1)
     high, low = split(local)
     grad_s[...] = dot(fw_s[...], jnp.concatenate([high, high, low], axis=0))
 
@@ -451,9 +453,9 @@
         for x in range(16):
             a_s[m, :, pl.ds(ROW * x, ROW)] = grid_s[m, x : x + 1, :ROW]
         a_s[m, :, pl.ds(ROW * 16, ROW)] = grid_s[3, m : m + 1, :ROW]
-    a_copy = pltpu.make_async_copy(a_s, a_out, sems.at[0])
+    a_copy = pltpu.make_async_copy(a_s.at[pl.ds(0, 3)], a_out, sems.at[0])
     a_copy.start()
-    v_s[...] = vh_ref[...] + HALF * a_s[...]
+    v_s[...] = vh_ref[...] + HALF * a_s[0:3]
     v_copy = pltpu.make_async_copy(v_s, v_out, sems.at[1])
     v_copy.start()
     a_copy.wait()
@@ -489,7 +491,7 @@
         pltpu.VMEM((128, 128), F32), pltpu.VMEM((128, 128), F32),
         pltpu.VMEM((384, 384), BF16), pltpu.VMEM((256, 384), BF16),
         pltpu.VMEM((4, 16, 640), F32), pltpu.VMEM((3, 7, 24, 128), F32),
-        pltpu.VMEM((3, 128, 128), F32), pltpu.VMEM((384, 384), F32),
+        pltpu.VMEM((3, 200, 128), F32), pltpu.VMEM((384, 384), F32), pltpu.VMEM((4, 1, NODES), F32),
         pltpu.VMEM((384, 384), BF16), pltpu.VMEM((384, 384), BF16),
         pltpu.SemaphoreType.DMA((25,)),
     ]
@@ -573,7 +575,7 @@
         in_specs=[VMEM] * 5,
         out_specs=(HBM, HBM),
         scratch_shapes=[
-            pltpu.VMEM(flat, F32), pltpu.VMEM(flat, F32), pltpu.VMEM((4, 2, 16, 128), F32),
+            pltpu.VMEM((4, 1, NODES), F32), pltpu.VMEM(flat, F32), pltpu.VMEM((4, 2, 16, 128), F32),
             pltpu.VMEM((4, 16, 640), F32), pltpu.SemaphoreType.DMA((2,)),
         ],
         compiler_params=pltpu.CompilerParams(vmem_limit_bytes=8 << 20),

time: 28.9 us -> 28.9 us (level)
  no operation moved by 1% of the time
where the time goes in v7:
time: 28.9 us; the launch traced here: 28.8 us
  starting transfers between devices  16.7 us (58%)
  Pallas kernels  8.06 us (28%)
  waiting for transfers between devices  3.31 us (11%)
  between operations  0.7 us (2%)
    ppermute x5, starting transfers between devices, swap(): return lax.ppermute(value, axes, pairs)  13.1 us
    pallas_call x1, Pallas kernels, body(): pl.pallas_call(force_kernel, out_shape=(f32((4, 200, 128)), jax.ShapeDtyp...  3.66 us
    ppermute x1, starting transfers between devices, body(): passed = lax.ppermute(ya, 'gy', hops)  3.63 us
    ppermute x5, waiting for transfers between devices, swap(): return lax.ppermute(value, axes, pairs)  3.31 us
    pallas_call x1, Pallas kernels, body(): pl.pallas_call(field_kernel, out_shape=f32((FROWS, 128)), in_specs=[VMEM]...  1.83 us
    pallas_call x1, Pallas kernels, body(): pl.pallas_call(end_kernel, out_shape=(f32(flat), f32(flat)), in_specs=[VM...  1.1 us
    pallas_call x1, Pallas kernels, body(): pl.pallas_call(inner_kernel, out_shape=(f32((4, 16, 640)), f32(flat), f32...  0.67 us
  transfers between devices with their start and end apart: 6, of which 3 were waited for; matrix products, arithmetic and copies ran while one was open for 0% of the time, Pallas kernels for 11%

profile of v7, /device:TPU:1, one launch (start us, length us, event | category | flops | bytes accessed | tf_op | source)
XLA Modules:
  0.0 28.8 jit_solution(12753137289182919889)
XLA Ops:
  0.6 3.7 %shard_map.130 = (f32[4,200,128]{2,1,0:T(8,128)S(1)}, s32[8,128]{1,0:T(8,128)S(1)}, f32[24,128]{1,0:T(8,128)S(1)}, f32[3,1,9945]{2,1,0:T(1,128)S(1)}, f32[3,1,99...) custom-call(f32[3,1,9945]{2,1,0:T(1,128)} %bitcast.19, f32[3,1,9945]{2,1,0:T(1,128)} %bitcast.20, f32[3,1,9945]{2,1,0:T(1,128)} %bitcast.21, ...), custom_call_target="tpu_custom_call" | custom-call | tf_op jit(solution)/shard_map/pallas_call | solution.py:498
  4.3 3.6 %collective-permute-start = (f32[24,128]{1,0:T(8,128)S(1)}, f32[24,128]{1,0:T(8,128)S(1)}, u32[]{:S(2)}, u32[]{:S(2)}) collective-permute-start(f32[24,128]{1,0:T(8,128)S(1)} %get-tuple-element.21), channel_id=1, source_target_pairs={{0,48},{8,24},{16,0},{24,40},{32,16},{40,56},{48,32},{56,8},{1,49}... | collective-permute-start | bytes 36872 | tf_op jit(solution)/shard_map/ppermute | solution.py:522
  7.9 1.8 %shard_map.131.f_ref.f_in = f32[960,128]{1,0:T(8,128)S(1)} custom-call(f32[4,200,128]{2,1,0:T(8,128)S(1)} %get-tuple-element.22.t_ref, s32[8,128]{1,0:T(8,128)S(1)} %get-tuple-element.23.o_ref), custom_call_target="tpu_custom_call" | custom-call | flops 4000000 | bytes 800000 | tf_op jit(solution)/shard_map/pallas_call | solution.py:523
  9.8 0.0 collective-permute-done
  9.8 6.1 %collective-permute-start.1 = (f32[24,128]{1,0:T(8,128)S(1)}, f32[24,128]{1,0:T(8,128)S(1)}, u32[]{:S(2)}, u32[]{:S(2)}) collective-permute-start(f32[24,128]{1,0:T(8,128)S(1)} %broadcast_select_fusion), channel_id=1, source_target_pairs={{0,8},{1,9},{2,10},{3,11},{4,12},{5,13},{6,14},{7,15},{8,0},{9,1},... | collective-permute-start | bytes 36872 | tf_op jit(solution)/shard_map/ppermute | solution.py:479
  15.9 1.1 %collective-permute-done.1.y_ref = f32[24,128]{1,0:T(8,128)S(1)} collective-permute-done((f32[24,128]{1,0:T(8,128)S(1)}, f32[24,128]{1,0:T(8,128)S(1)}, u32[]{:S(2)}, u32[]{:S(2)}) %collective-permute-start.1) | collective-permute-done | bytes 12320 | tf_op jit(solution)/shard_map/ppermute | solution.py:479
  17.0 0.2 shard_map.132
  17.2 1.0 %collective-permute-start.2 = (f32[40,128]{1,0:T(8,128)S(1)}, f32[40,128]{1,0:T(8,128)S(1)}, u32[]{:S(2)}, u32[]{:S(2)}) collective-permute-start(f32[40,128]{1,0:T(8,128)S(1)} %get-tuple-element.26), channel_id=1, source_target_pairs={{0,64},{1,65},{2,66},{3,67},{4,68},{5,69},{6,70},{7,71},{8,72},{9,... | collective-permute-start | bytes 61448 | tf_op jit(solution)/shard_map/ppermute | solution.py:479
  18.2 2.7 %collective-permute-start.3 = (f32[40,128]{1,0:T(8,128)S(1)}, f32[40,128]{1,0:T(8,128)S(1)}, u32[]{:S(2)}, u32[]{:S(2)}) collective-permute-start(f32[40,128]{1,0:T(8,128)S(1)} %get-tuple-element.27), channel_id=1, source_target_pairs={{0,1},{1,0},{2,3},{3,2},{4,5},{5,4},{6,7},{7,6},{8,9},{9,8},{10,11... | collective-permute-start | bytes 61448 | tf_op jit(solution)/shard_map/ppermute | solution.py:479
  20.9 0.5 %shard_map.133.f_in = f32[960,128]{1,0:T(8,128)S(1)} custom-call(f32[24,128]{1,0:T(8,128)S(1)} %collective-permute-done.1.y_ref, f32[960,128]{1,0:T(8,128)S(1)} %shard_map.131.f_ref.f_in), custom_call_target="tpu_custom_call", output_to_operand_aliasing={{}: (1, {})} | custom-call | flops 1000000 | bytes 800000 | tf_op jit(solution)/shard_map/pallas_call | solution.py:541
  21.5 0.0 collective-permute-done.2.xa_ref
  21.5 0.3 %collective-permute-done.3.xb_ref = f32[40,128]{1,0:T(8,128)S(1)} collective-permute-done((f32[40,128]{1,0:T(8,128)S(1)}, f32[40,128]{1,0:T(8,128)S(1)}, u32[]{:S(2)}, u32[]{:S(2)}) %collective-permute-start.3) | collective-permute-done | bytes 20512 | tf_op jit(solution)/shard_map/ppermute | solution.py:479
  21.8 0.1 shard_map.134
  21.9 2.0 %collective-permute-start.4 = (f32[96,128]{1,0:T(8,128)S(1)}, f32[96,128]{1,0:T(8,128)S(1)}, u32[]{:S(2)}, u32[]{:S(2)}) collective-permute-start(f32[96,128]{1,0:T(8,128)S(1)} %get-tuple-element.33), channel_id=1, source_target_pairs={{0,1},{1,0},{2,3},{3,2},{4,5},{5,4},{6,7},{7,6},{8,9},{9,8},{10,11... | collective-permute-start | bytes 147464 | tf_op jit(solution)/shard_map/ppermute | solution.py:479
  23.9 1.2 %collective-permute-start.5 = (f32[96,128]{1,0:T(8,128)S(1)}, f32[96,128]{1,0:T(8,128)S(1)}, u32[]{:S(2)}, u32[]{:S(2)}) collective-permute-start(f32[96,128]{1,0:T(8,128)S(1)} %get-tuple-element.34), channel_id=1, source_target_pairs={{0,64},{1,2},{2,1},{3,4},{4,3},{5,6},{6,5},{7,71},{8,72},{9,10},{1... | collective-permute-start | bytes 147464 | tf_op jit(solution)/shard_map/ppermute | solution.py:479
  25.1 0.7 %shard_map.135 = (f32[4,16,640]{2,1,0:T(8,128)S(1)}, f32[3,1,9945]{2,1,0:T(1,128)S(1)}, f32[3,1,9945]{2,1,0:T(1,128)}) custom-call(f32[960,128]{1,0:T(8,128)S(1)} %get-tuple-element.28.f_ref, f32[3,1,9945]{2,1,0:T(1,128)S(1)} %get-tuple-element.29.d_ref, f32[3,1,9945]{2,1,0:T(1,128)S(1)} %get-tuple-element.30.v_ref, f32[3,1,9945]{2,1,0:T(1,128)S(1)} %get-tuple-element.31.a_ref), custom_call_target="tpu_custom_call" | custom-call | flops 1000000 | bytes 800000 | tf_op jit(solution)/shard_map/pallas_call | solution.py:563
  25.8 0.0 collective-permute-done.4.za_ref
  25.8 1.9 %collective-permute-done.5.zb_ref = f32[96,128]{1,0:T(8,128)S(1)} collective-permute-done((f32[96,128]{1,0:T(8,128)S(1)}, f32[96,128]{1,0:T(8,128)S(1)}, u32[]{:S(2)}, u32[]{:S(2)}) %collective-permute-start.5) | collective-permute-done | bytes 49184 | tf_op jit(solution)/shard_map/ppermute | solution.py:479
  27.7 1.1 %shard_map.136 = (f32[3,1,9945]{2,1,0:T(1,128)}, f32[3,1,9945]{2,1,0:T(1,128)}) custom-call(f32[96,128]{1,0:T(8,128)S(1)} %collective-permute-done.4.za_ref, f32[96,128]{1,0:T(8,128)S(1)} %collective-permute-done.5.zb_ref, f32[960,128]{1,0:T(8,128)S(1)} %get-tuple-element.28.f_ref, f32[3,1,9945]{2,1,0:T(1,128)S(1)} %get-tuple-element.35.vh_ref, ...), custom_call_target="tpu_custom_call" | custom-call | tf_op jit(solution)/shard_map/pallas_call | solution.py:572
  (2 shorter events, 0.0 us)
Async XLA Ops:
  4.3 5.5 %collective-permute-start = (f32[24,128]{1,0:T(8,128)S(1)}, f32[24,128]{1,0:T(8,128)S(1)}, u32[]{:S(2)}, u32[]{:S(2)}) collective-permute-start(f32[24,128]{1,0:T(8,128)S(1)} %get-tuple-element.21), channel_id=1, source_target_pairs={{0,48},{8,24},{16,0},{24,40},{32,16},{40,56},{48,32},{56,8},{1,49}... | collective-permute-start | bytes 36872 | tf_op jit(solution)/shard_map/ppermute | solution.py:522
  9.8 7.2 %collective-permute-start.1 = (f32[24,128]{1,0:T(8,128)S(1)}, f32[24,128]{1,0:T(8,128)S(1)}, u32[]{:S(2)}, u32[]{:S(2)}) collective-permute-start(f32[24,128]{1,0:T(8,128)S(1)} %broadcast_select_fusion), channel_id=1, source_target_pairs={{0,8},{1,9},{2,10},{3,11},{4,12},{5,13},{6,14},{7,15},{8,0},{9,1},... | collective-permute-start | bytes 36872 | tf_op jit(solution)/shard_map/ppermute | solution.py:479
  17.2 4.3 %collective-permute-start.2 = (f32[40,128]{1,0:T(8,128)S(1)}, f32[40,128]{1,0:T(8,128)S(1)}, u32[]{:S(2)}, u32[]{:S(2)}) collective-permute-start(f32[40,128]{1,0:T(8,128)S(1)} %get-tuple-element.26), channel_id=1, source_target_pairs={{0,64},{1,65},{2,66},{3,67},{4,68},{5,69},{6,70},{7,71},{8,72},{9,... | collective-permute-start | bytes 61448 | tf_op jit(solution)/shard_map/ppermute | solution.py:479
  18.2 3.5 %collective-permute-start.3 = (f32[40,128]{1,0:T(8,128)S(1)}, f32[40,128]{1,0:T(8,128)S(1)}, u32[]{:S(2)}, u32[]{:S(2)}) collective-permute-start(f32[40,128]{1,0:T(8,128)S(1)} %get-tuple-element.27), channel_id=1, source_target_pairs={{0,1},{1,0},{2,3},{3,2},{4,5},{5,4},{6,7},{7,6},{8,9},{9,8},{10,11... | collective-permute-start | bytes 61448 | tf_op jit(solution)/shard_map/ppermute | solution.py:479
  21.9 3.9 %collective-permute-start.4 = (f32[96,128]{1,0:T(8,128)S(1)}, f32[96,128]{1,0:T(8,128)S(1)}, u32[]{:S(2)}, u32[]{:S(2)}) collective-permute-start(f32[96,128]{1,0:T(8,128)S(1)} %get-tuple-element.33), channel_id=1, source_target_pairs={{0,1},{1,0},{2,3},{3,2},{4,5},{5,4},{6,7},{7,6},{8,9},{9,8},{10,11... | collective-permute-start | bytes 147464 | tf_op jit(solution)/shard_map/ppermute | solution.py:479
  23.9 3.8 %collective-permute-start.5 = (f32[96,128]{1,0:T(8,128)S(1)}, f32[96,128]{1,0:T(8,128)S(1)}, u32[]{:S(2)}, u32[]{:S(2)}) collective-permute-start(f32[96,128]{1,0:T(8,128)S(1)} %get-tuple-element.34), channel_id=1, source_target_pairs={{0,64},{1,2},{2,1},{3,4},{4,3},{5,6},{6,5},{7,71},{8,72},{9,10},{1... | collective-permute-start | bytes 147464 | tf_op jit(solution)/shard_map/ppermute | solution.py:479
